TPU v7x, 128 devices: a whole 4x4x4 slice. The times are simulated.
128 devices in a mesh: dp: 32 (over y, z, core), mp: 4 (over x).
Axes of the slice: x: 4, y: 4, z: 4, core: 2. Of those that a mesh axis runs over, the one named last changes fastest.
Arguments:
- pred_input: bfloat16 [2048, 256, 384], P('dp'), may hold values from -6 to 6
- proj_weight: bfloat16 [384, 1280], P('dp', 'mp'), may hold values from -0.3125 to 0.3125
- proj_bias: float32 [1280], P('mp'), may hold values from -3 to 3
- targets: bfloat16 [2048, 256, 1280], P('dp', None, 'mp'), may hold values from -6 to 6
- block_masks: int32 [2048, 4, 256], P('dp'), may hold values from 0 to 1, as said below
Outputs:
- loss: float32 [], replicated
- clip_scale: float32 [], replicated
- grad_weight: float32 [384, 1280], P('dp', 'mp')
- grad_bias: float32 [1280], P('mp')
Inputs may be any that keep to these rules, and one draw needn't show every extreme that they name: `block_masks`: each of an image's 4 target blocks is a nonempty rectangle of patches on the 16 x 16 grid (row-major patch order); blocks may intersect.
All inputs are finite; a program needn't handle non-finite values.
Results may differ from a plain program's by a relative error of at most 0.0003.
Values may be sent and summed in bfloat16 or wider, within the bound.
A program may use at most 192 MiB of HBM per device.

v0:
```python
import functools

import jax
import jax.numpy as jnp
from jax import lax
from jax.sharding import Mesh
from jax.sharding import PartitionSpec as P

DP = ("dp_0", "dp_1", "dp_2")
DP_MP = ("dp_0", "dp_1", "dp_2", "mp")


def copy_for_each(value, axis):
    copies = jnp.broadcast_to(value, (lax.axis_size(axis), *value.shape))
    return lax.all_to_all(copies, axis, split_axis=0, concat_axis=0, tiled=True)


def of_everyone(value, axis):
    everything = copy_for_each(value, axis)
    return jnp.sum(everything, axis=0)


def in_one(arrays, axis):
    flat, at, done = (jnp.concatenate([a.reshape(-1) for a in arrays]), 0, [])
    running = of_everyone(flat, axis)
    for a in arrays:
        done.append(running[at : at + a.size].reshape(a.shape))
        at += a.size
    return tuple(done)


def in_order(parts, dim):
    parts = jnp.moveaxis(parts, 0, dim)
    dims = parts.shape
    return parts.reshape(*dims[:dim], dims[dim] * dims[dim + 1], *dims[dim + 2 :])


def gathered_copies(value, axis, dim):
    return in_order(copy_for_each(value, axis), dim)


def cut_along(value, dim, size):
    dims = value.shape
    parts = value.reshape(*dims[:dim], size, dims[dim] // size, *dims[dim + 1 :])
    return jnp.moveaxis(parts, dim, 0)


def sum_at_owner(value, axis, dim):
    parts = cut_along(value, dim, lax.axis_size(axis))
    arrived = lax.all_to_all(parts, axis, split_axis=0, concat_axis=0, tiled=True)
    return arrived.sum(axis=0)


def one_axis_at_a_time(value, axes):
    return functools.reduce(lax.psum, axes, value)


def body(pred_input, proj_weight, proj_bias, targets, block_masks):
    images_here, patches, pred_width = pred_input.shape
    feat_local = targets.shape[2]
    feat_full = feat_local * lax.axis_size("mp")
    token_count = images_here * patches
    coverage = jnp.sum(block_masks, axis=1).astype(jnp.float32)
    share = patches // lax.axis_size("mp")
    owned_cover = lax.dynamic_slice_in_dim(coverage, lax.axis_index("mp") * share, share, 1)
    count_part = jnp.sum(owned_cover)
    target_f = targets.astype(jnp.float32).reshape(token_count, feat_local)
    feat_sums, feat_squares = in_one(
        (jnp.sum(target_f, axis=1), jnp.sum(target_f * target_f, axis=1)), "mp"
    )
    mean_feat = feat_sums / feat_full
    variance = feat_squares / feat_full - mean_feat * mean_feat
    tnorm = (target_f - mean_feat[:, None]) * lax.rsqrt(variance[:, None] + 1e-05)
    inputs_flat = pred_input.reshape(token_count, pred_width)
    weight_full = gathered_copies(proj_weight, DP, 0)
    pred = jnp.dot(inputs_flat, weight_full, preferred_element_type=jnp.float32) + proj_bias
    differ = pred - tnorm
    magnitude = jnp.abs(differ)
    smooth = jnp.where(magnitude < 1.0, 0.5 * differ * differ, magnitude - 0.5)
    cover_column = coverage.reshape(token_count, 1)
    loss_part = jnp.sum(cover_column * smooth)
    clipped = cover_column * jnp.clip(differ, -1.0, 1.0)
    source = clipped.astype(jnp.bfloat16)
    grad_full = lax.dot_general(
        inputs_flat, source, (((0,), (0,)), ((), ())), preferred_element_type=jnp.float32
    )
    bias_part = jnp.sum(clipped, axis=0)
    grad_rows = sum_at_owner(grad_full, DP, 0)
    bias_grad = of_everyone(bias_part, DP)
    bias_square = jnp.where(lax.axis_index(DP) == 0, jnp.sum(bias_grad * bias_grad), 0.0)
    square_part = jnp.sum(grad_rows * grad_rows) + bias_square
    total, loss_total, square_total = (
        one_axis_at_a_time(count_part, DP_MP),
        one_axis_at_a_time(loss_part, DP_MP),
        one_axis_at_a_time(square_part, DP_MP),
    )
    norm = jnp.sqrt(square_total) / total
    clip_scale = jnp.minimum(1.0, 1.0 / (norm + 1e-06))
    factor = clip_scale / total
    loss = loss_total / total / feat_full
    return (loss, clip_scale, grad_rows * factor, bias_grad * factor)


def solution(mesh):
    split = Mesh(mesh.devices.reshape(4, 4, 2, mesh.shape["mp"]), ("dp_0", "dp_1", "dp_2", "mp"))
    return jax.shard_map(
        body,
        mesh=split,
        in_specs=(P(DP, None, None), P(DP, "mp"), P("mp"), P(DP, None, "mp"), P(DP, None, None)),
        out_specs=(P(), P(), P(DP, "mp"), P("mp")),
        check_vma=False,
    )
```

profile of v0, /device:TPU:1, one launch (start us, length us, event | category | flops | bytes accessed | tf_op | source)
XLA Modules:
  0.0 168.1 jit_solution(16816009455402599750)
XLA Ops:
  0.6 1.5 broadcast_in_dim.12
  2.1 9.6 %all-to-all-start = ((bf16[32,12,320]{2,1,0:T(8,128)(2,1)}), bf16[32,12,320]{2,1,0:T(8,128)(2,1)S(1)}, u32[]{:S(2)}, u32[]{:S(2)}) async-start(bf16[32,12,320]{2,1,0:T(8,128)(2,1)} %broadcast_in_dim.12), calls=%async_computation | async-start | bytes 786432 | tf_op jit(solution)/shard_map/all_to_all | solution.py:15
  11.7 0.0 copy-start
  11.7 9.9 %convert_reduce_fusion = (f32[64,256]{1,0:T(8,128)S(1)}, f32[64,256]{1,0:T(8,128)S(1)}) fusion(bf16[64,256,320]{1,2,0:T(8,128)(2,1)} %param.8), kind=kLoop, calls=%fused_computation.2 | loop fusion | flops 20938752 | bytes 10616832 | tf_op jit(solution)/shard_map/reduce_sum | solution.py:69
  21.8 0.2 all-to-all-done
  22.0 1.1 broadcast_in_dim.13
  23.1 4.0 %all-to-all-start.1 = ((f32[4,1,32768]{2,1,0:T(1,128)}), f32[4,1,32768]{2,1,0:T(1,128)S(1)}, u32[]{:S(2)}, u32[]{:S(2)}) async-start(f32[4,1,32768]{2,1,0:T(1,128)} %broadcast_in_dim.13), calls=%async_computation.1 | async-start | bytes 1048576 | tf_op jit(solution)/shard_map/all_to_all | solution.py:15
  27.1 13.8 %convert_bitcast_fusion = f32[64,40,8,256]{3,2,1,0:T(8,128)} fusion(bf16[64,256,320]{1,2,0:T(8,128)(2,1)} %param.8), kind=kLoop, calls=%fused_computation.3 | loop fusion | flops 5242880 | bytes 31457280
  40.9 0.2 reduce_sum.103
  41.1 0.0 copy-start.1
  41.1 15.8 %copy.22 = f32[64,40,8,256]{3,2,0,1:T(8,128)} copy(f32[64,40,8,256]{3,2,1,0:T(8,128)} %convert_bitcast_fusion) | data formatting | bytes 41943040 | tf_op jit(solution)/shard_map/reshape | solution.py:67
  57.0 0.1 reshape.43
  57.1 0.5 reduce_sum.108
  57.7 26.1 %fusion.5 = (f32[320]{0:T(512)S(1)}, f32[]{:T(128)}, f32[16384,320]{0,1:T(8,128)}) fusion(f32[16384]{0:T(1024)S(1)} %bitcast.19, f32[16384]{0:T(1024)S(1)} %get-tuple-element.21, f32[16384,320]{0,1:T(8,128)} %bitcast.18, f32[16384]{0:T(1024)S(1)} %get-tuple-element.20, f32[320]{0:T(512)S(1)} %copy-done.1, bf16[16384,384]{1,0:T(8,128)(2,1)} %bitcast.16, ...), kind=kOutput, calls=%fused_computation.11 | convolution fusion | flops 4105174784 | bytes 54970884 | tf_op jit(solution)/shard_map/dot_general | solution.py:76
  83.8 0.6 broadcast_in_dim.14
  84.4 7.5 %all-to-all-start.3 = ((f32[32,1,320]{2,1,0:T(1,128)}), f32[32,1,320]{2,1,0:T(1,128)S(1)}, u32[]{:S(2)}, u32[]{:S(2)}) async-start(f32[32,1,320]{2,1,0:T(1,128)} %broadcast_in_dim.14), calls=%async_computation.3 | async-start | bytes 98304 | tf_op jit(solution)/shard_map/all_to_all | solution.py:15
  91.9 13.5 %fusion.12 = f32[384,320]{0,1:T(8,128)S(1)} fusion(bf16[16384,384]{1,0:T(8,128)(2,1)} %bitcast.17, f32[16384,320]{0,1:T(8,128)} %get-tuple-element.24, f32[16384]{0:T(1024)S(1)} %bitcast.20), kind=kOutput, calls=%fused_computation.17 | convolution fusion | flops 4042260480 | bytes 34111488 | tf_op jit(solution)/shard_map/dot_general | solution.py:84
  105.3 0.2 copy.16
  105.6 0.9 reshape.45
  106.5 7.4 %all-to-all-start.2 = ((f32[32,12,320]{2,1,0:T(8,128)}), f32[32,12,320]{2,1,0:T(8,128)S(1)}, u32[]{:S(2)}, u32[]{:S(2)}) async-start(f32[32,12,320]{2,1,0:T(8,128)} %reshape.45), calls=%async_computation.2 | async-start | bytes 1572864 | tf_op jit(solution)/shard_map/all_to_all | solution.py:50
  113.9 0.7 dynamic-slice_reduce_fusion
  114.6 0.1 reduce_sum.114
  114.7 0.6 multiply_reduce_fusion.1
  115.9 12.2 %all-to-all-done.2 = f32[32,12,320]{2,1,0:T(8,128)S(1)} async-done(((f32[32,12,320]{2,1,0:T(8,128)}), f32[32,12,320]{2,1,0:T(8,128)S(1)}, u32[]{:S(2)}, u32[]{:S(2)}) %all-to-all-start.2) | async-done | bytes 491552 | tf_op jit(solution)/shard_map/all_to_all | solution.py:50
  128.1 0.1 reduce_sum.111
  128.2 0.6 multiply_reduce_fusion
  129.5 7.2 %all-reduce.2 = (f32[]{:T(128)}, f32[]{:T(128)}, f32[]{:T(128)}) all-reduce(f32[]{:T(128)} %get-tuple-element.5, f32[]{:T(128)} %dynamic-slice_reduce_fusion, f32[]{:T(128)S(6)} %add.62), channel_id=1, replica_groups=mesh['dp_0'=4,'dp_1'=4,'dp_2'=2,'mp'=4] {'dp_0'}, use_global_device_ids=true, to_apply=%region_5.6 | all-reduce | flops 3 | bytes 24 | tf_op jit(solution)/shard_map/psum | solution.py:55
  136.6 8.1 %all-reduce.1 = (f32[]{:T(128)}, f32[]{:T(128)}, f32[]{:T(128)}) all-reduce(f32[]{:T(128)} %get-tuple-element.14, f32[]{:T(128)} %get-tuple-element.15, f32[]{:T(128)} %get-tuple-element.16), channel_id=1, replica_groups=mesh['dp_0'=4,'dp_1'=4,'dp_2'=2,'mp'=4] {'dp_1'}, use_global_device_ids=true, to_apply=%region_6.7 | all-reduce | flops 3 | bytes 24 | tf_op jit(solution)/shard_map/psum | solution.py:55
  144.7 6.8 %all-reduce.3 = (f32[]{:T(128)}, f32[]{:T(128)}, f32[]{:T(128)}) all-reduce(f32[]{:T(128)} %get-tuple-element.11, f32[]{:T(128)} %get-tuple-element.12, f32[]{:T(128)} %get-tuple-element.13), channel_id=1, replica_groups=mesh['dp_0'=4,'dp_1'=4,'dp_2'=2,'mp'=4] {'dp_2'}, use_global_device_ids=true, to_apply=%region_7.8 | all-reduce | flops 3 | bytes 24 | tf_op jit(solution)/shard_map/psum | solution.py:55
  151.6 9.6 %all-reduce = (f32[]{:T(128)}, f32[]{:T(128)}, f32[]{:T(128)}) all-reduce(f32[]{:T(128)} %get-tuple-element.17, f32[]{:T(128)} %get-tuple-element.18, f32[]{:T(128)} %get-tuple-element.19), channel_id=1, replica_groups=mesh['dp_0'=4,'dp_1'=4,'dp_2'=2,'mp'=4] {'mp'}, use_global_device_ids=true, to_apply=%region_8.9 | all-reduce | flops 3 | bytes 24 | tf_op jit(solution)/shard_map/psum | solution.py:55
  163.3 0.6 broadcast_multiply_fusion.1
  163.9 0.6 broadcast_multiply_fusion
  (10 shorter events, 0.2 us)
Async XLA Ops:
  2.1 19.9 %all-to-all-start = ((bf16[32,12,320]{2,1,0:T(8,128)(2,1)}), bf16[32,12,320]{2,1,0:T(8,128)(2,1)S(1)}, u32[]{:S(2)}, u32[]{:S(2)}) async-start(bf16[32,12,320]{2,1,0:T(8,128)(2,1)} %broadcast_in_dim.12), calls=%async_computation | async-start | bytes 786432 | tf_op jit(solution)/shard_map/all_to_all | solution.py:15
  11.7 29.2 %copy-start = (s32[64,4,256]{2,1,0:T(4,128)S(1)}, s32[64,4,256]{2,1,0:T(4,128)}, u32[]{:S(2)}) copy-start(s32[64,4,256]{2,1,0:T(4,128)} %param.9) | copy-start | bytes 786436
  23.1 34.1 %all-to-all-start.1 = ((f32[4,1,32768]{2,1,0:T(1,128)}), f32[4,1,32768]{2,1,0:T(1,128)S(1)}, u32[]{:S(2)}, u32[]{:S(2)}) async-start(f32[4,1,32768]{2,1,0:T(1,128)} %broadcast_in_dim.13), calls=%async_computation.1 | async-start | bytes 1048576 | tf_op jit(solution)/shard_map/all_to_all | solution.py:15
  41.1 16.5 %copy-start.1 = (f32[320]{0:T(512)S(1)}, f32[320]{0:T(512)}, u32[]{:S(2)}) copy-start(f32[320]{0:T(512)} %param.7) | copy-start | bytes 3844
  84.4 22.1 %all-to-all-start.3 = ((f32[32,1,320]{2,1,0:T(1,128)}), f32[32,1,320]{2,1,0:T(1,128)S(1)}, u32[]{:S(2)}, u32[]{:S(2)}) async-start(f32[32,1,320]{2,1,0:T(1,128)} %broadcast_in_dim.14), calls=%async_computation.3 | async-start | bytes 98304 | tf_op jit(solution)/shard_map/all_to_all | solution.py:15
  106.5 21.6 %all-to-all-start.2 = ((f32[32,12,320]{2,1,0:T(8,128)}), f32[32,12,320]{2,1,0:T(8,128)S(1)}, u32[]{:S(2)}, u32[]{:S(2)}) async-start(f32[32,12,320]{2,1,0:T(8,128)} %reshape.45), calls=%async_computation.2 | async-start | bytes 1572864 | tf_op jit(solution)/shard_map/all_to_all | solution.py:50
where the time goes:
time: 170 us; the launch traced here: 168 us
  matrix products  39.6 us (23%)
  blocking collectives  31.7 us (19%)
  starting transfers between devices  28.4 us (17%)
  other arithmetic  27.7 us (16%)
  local copies, waits for them, and re-layouts  20.5 us (12%)
  waiting for transfers between devices  12.4 us (7%)
  between operations  7.84 us (5%)
    psum x4, blocking collectives, one_axis_at_a_time(): return functools.reduce(lax.psum, axes, value)  31.7 us
    dot_general x1, matrix products, body(): jnp.dot(inputs_flat, weight_full, preferred_element_type=jnp.float32)  26.1 us
    all_to_all x3, starting transfers between devices, copy_for_each(): return lax.all_to_all(copies, axis, split_axis=0, concat_axis=0, tiled=True)  21.1 us
    reshape x1, local copies, waits for them, and re-layouts, body(): target_f = targets.astype(jnp.float32).reshape(token_count, feat_local)  15.8 us
    unnamed x1, other arithmetic  13.8 us
    dot_general x1, matrix products, body(): lax.dot_general(inputs_flat, source, (((0,), (0,)), ((), ())), preferred_...  13.5 us
    all_to_all x1, waiting for transfers between devices, sum_at_owner(): lax.all_to_all(parts, axis, split_axis=0, concat_axis=0, tiled=True)  12.2 us
    reduce_sum x1, other arithmetic, body(): jnp.sum(target_f, axis=1)  9.94 us
  transfers between devices with their start and end apart: 4, of which 2 were waited for; matrix products, arithmetic and copies ran while one was open for 33% of the time, Pallas kernels for 0%

commit v1 on v0

v1 whole, which is shorter than its diff:
```python
import jax
import jax.numpy as jnp
from jax import lax
from jax.experimental import pallas as pl
from jax.experimental.pallas import tpu as pltpu
from jax.sharding import PartitionSpec as P

MESH = pl.DeviceIdType.MESH
F32 = jnp.float32
BF16 = jnp.bfloat16

NY, NZ, NC, NX = 4, 4, 2, 4
NCHIP = NY * NZ
NDP = NCHIP * NC
GI = 4
NG = 16
IMG = GI * NG
PAT = 256
FEAT = 320
FULL = FEAT * NX
E = 384
ROWS = E // NDP
FP = 384
RB = 64
EARLY = 6

OFFSETS = sorted(
    [(dy, dz) for dy in range(NY) for dz in range(NZ) if (dy, dz) != (0, 0)],
    key=lambda o: -(min(o[0], NY - o[0]) + min(o[1], NZ - o[1])),
)


def kernel(
    x_hbm, w_hbm, b_hbm, t_hbm, m_hbm,
    loss_o, clip_o, gw_o, gb_o,
    xv, tv, mv, wi, wtmp, wg, wsq, wt, bi, bias, pm,
    st_own, st_in, ab, cb, vb, pscr, sscr, acc, gbt, lacc, gt, sb, pin, ps, rr, na, nb,
    x_sem, t_sem, misc_sem,
    st_send, st_recv, w_send, w_recv, c_send, c_recv, r_send, r_recv, a_send, a_recv, b_send, b_recv,
):
    me = lax.axis_index("dp")
    mx = lax.axis_index("mp")
    core = lax.rem(me, NC)
    chip = lax.div(me, NC)
    my_y = lax.div(chip, NZ)
    my_z = lax.rem(chip, NZ)
    partner = me + 1 - 2 * core

    def chip_at(dy, dz):
        return lax.rem(my_y + dy, NY) * NZ + lax.rem(my_z + dz, NZ)

    w_copy = pltpu.make_async_copy(w_hbm, wi, misc_sem.at[0])
    w_copy.start()

    def t_copy(g):
        return pltpu.make_async_copy(
            t_hbm.at[pl.ds(g * GI, GI)], tv.at[pl.ds(g * GI, GI)], t_sem.at[g]
        )

    def x_copy(g):
        return pltpu.make_async_copy(
            x_hbm.at[pl.ds(g * GI, GI)], xv.at[pl.ds(g * GI, GI)], x_sem.at[g]
        )

    def start_t(g, _):
        t_copy(g).start()
        return 0

    lax.fori_loop(0, NG, start_t, 0)
    m_copy = pltpu.make_async_copy(m_hbm, mv, misc_sem.at[1])
    m_copy.start()
    b_copy = pltpu.make_async_copy(b_hbm, bi, misc_sem.at[2])
    b_copy.start()

    barrier = pltpu.get_barrier_semaphore()
    for dy, dz in OFFSETS:
        for c in range(NC):
            pl.semaphore_signal(
                barrier, inc=1, device_id=(chip_at(dy, dz) * NC + c, mx), device_id_type=MESH
            )
    pl.semaphore_signal(barrier, inc=1, device_id=(partner, mx), device_id_type=MESH)
    for dx in range(1, NX):
        for c in range(NC):
            pl.semaphore_signal(
                barrier, inc=1,
                device_id=(chip * NC + c, lax.rem(mx + dx, NX)), device_id_type=MESH,
            )

    w_copy.wait()
    wtmp[...] = jnp.zeros_like(wtmp)
    wtmp[0:ROWS, :] = wi[...].astype(F32)
    wg[me] = wtmp[...].astype(BF16)
    b_copy.wait()

    row = lax.broadcasted_iota(jnp.int32, (E, NDP * 16), 0)
    col = lax.broadcasted_iota(jnp.int32, (E, NDP * 16), 1)
    low = lax.bitwise_and(col, 15)
    pick = (row == lax.shift_right_logical(col, 4) * ROWS + low) & (low < ROWS)
    pm[...] = jnp.where(pick, 1.0, 0.0).astype(BF16)
    wsq[...] = jnp.zeros_like(wsq)
    wsq[0:8, 0:FEAT] = jnp.broadcast_to(bi[...], (8, FEAT))
    bcol = jnp.transpose(jnp.broadcast_to(wsq[0:1, :], (128, FP)))
    bias[...] = bcol[0:FEAT, :]
    acc[...] = jnp.zeros_like(acc)
    gbt[...] = jnp.zeros_like(gbt)
    lacc[...] = jnp.zeros_like(lacc)
    sscr[...] = jnp.zeros_like(sscr)

    def stats(g):
        t_copy(g).wait()
        x_copy(g).start()
        sums, squares = [], []
        for k in range(GI):
            s8 = jnp.zeros((8, PAT), F32)
            q8 = jnp.zeros((8, PAT), F32)
            for r in range(0, FEAT, RB):
                t = tv[g * GI + k, r : r + RB, :].astype(F32).reshape(RB // 8, 8, PAT)
                s8 = s8 + jnp.sum(t, axis=0)
                q8 = q8 + jnp.sum(t * t, axis=0)
            sums.append(jnp.sum(s8, axis=0, keepdims=True))
            squares.append(jnp.sum(q8, axis=0, keepdims=True))
        st_own[g] = jnp.concatenate(sums + squares, axis=0)

    def st_copy(g, p):
        return pltpu.make_async_remote_copy(
            src_ref=st_own.at[g],
            dst_ref=st_in.at[p - 1, g],
            send_sem=st_send.at[p - 1, g],
            recv_sem=st_recv.at[p - 1, g],
            device_id=(me, lax.rem(mx + p, NX)),
            device_id_type=MESH,
        )

    def send_stats(g):
        for p in (2, 1, 3):
            st_copy(g, p).start()

    def stats_only(g, _):
        stats(g)
        return 0

    lax.fori_loop(0, EARLY, stats_only, 0)
    pl.semaphore_wait(barrier, (NCHIP - 1) * NC + 1 + (NX - 1) * NC)

    def w_dst(n):
        return pltpu.make_async_remote_copy(
            src_ref=wg.at[me],
            dst_ref=wg.at[me],
            send_sem=w_send,
            recv_sem=w_recv,
            device_id=(n, mx),
            device_id_type=MESH,
        )

    for dy, dz in OFFSETS:
        for c in range(NC):
            w_dst(chip_at(dy, dz) * NC + c).start()
    w_dst(partner).start()

    def send_early(g, _):
        send_stats(g)
        return 0

    lax.fori_loop(0, EARLY - 1, send_early, 0)

    def stats_and_send(g, _):
        stats(g)
        send_stats(g - 1)
        return 0

    lax.fori_loop(EARLY, NG, stats_and_send, 0)

    m_copy.wait()

    def cover(i, total):
        v = jnp.sum(mv[i].astype(F32), axis=0, keepdims=True)
        vb[i] = jnp.broadcast_to(v, (8, PAT))
        return total + v

    counts = lax.fori_loop(0, IMG, cover, jnp.zeros((1, PAT), F32))
    send_stats(NG - 1)

    def prepare(g):
        for p in (1, 2, 3):
            st_copy(g, p).wait_recv()
        st = (st_own[g] + st_in[0, g]) + (st_in[1, g] + st_in[2, g])
        mean = st[0:GI] * (1.0 / FULL)
        var = jnp.maximum(st[GI : 2 * GI] * (1.0 / FULL) - mean * mean, 0.0)
        a = lax.rsqrt(var + 1e-05)
        c = mean * a
        for k in range(GI):
            ab[g * GI + k] = jnp.broadcast_to(a[k : k + 1], (8, PAT))
            cb[g * GI + k] = jnp.broadcast_to(c[k : k + 1], (8, PAT))

    whole = wg.at[pl.ds(0, NDP - 1)]
    pltpu.make_async_copy(whole, whole, w_recv).wait()
    pltpu.make_async_copy(whole, whole, w_send).wait()

    wsq[:, 0:FEAT] = jnp.dot(
        pm[...], wg[...].reshape(NDP * 16, FEAT), preferred_element_type=F32
    )
    wt[...] = jnp.transpose(wsq[...])[0:FEAT, :].astype(BF16)

    def first(g):
        for k in range(GI):
            pscr[:, k * PAT : (k + 1) * PAT] = lax.dot_general(
                wt[...], xv[g * GI + k], (((1,), (1,)), ((), ())), preferred_element_type=F32
            )

    def second(g):
        xs = xv[pl.ds(g * GI, GI)].reshape(GI * PAT, E)
        acc[0:FEAT, 0:E] += jnp.dot(sscr[...], xs, preferred_element_type=F32)

    def middle(g):
        loss8 = jnp.zeros((8, PAT), F32)
        for r in range(0, FEAT, RB):
            bb = bias[r : r + RB, :]
            b2 = jnp.concatenate([bb, bb], axis=1).reshape(RB // 8, 8, PAT)
            gsum = jnp.zeros((RB // 8, 8, PAT), F32)
            for k in range(GI):
                i = g * GI + k
                a = ab[i][None]
                c = cb[i][None]
                v = vb[i][None]
                p = pscr[r : r + RB, k * PAT : (k + 1) * PAT].reshape(RB // 8, 8, PAT)
                t = tv[i, r : r + RB, :].astype(F32).reshape(RB // 8, 8, PAT)
                d = (p + b2) - (t * a - c)
                h = jnp.minimum(jnp.maximum(d, -1.0), 1.0)
                s = v * h
                loss8 = loss8 + jnp.sum(s * (d - 0.5 * h), axis=0)
                gsum = gsum + s
                sscr[r : r + RB, k * PAT : (k + 1) * PAT] = s.reshape(RB, PAT).astype(BF16)
            gs = gsum.reshape(RB, PAT)
            acc[r : r + RB, E : E + 128] += gs[:, 0:128] + gs[:, 128:256]
        lacc[...] += loss8

    x_copy(0).wait()
    first(0)
    prepare(0)

    def main(g, _):
        nxt = jnp.minimum(g + 1, NG - 1)

        @pl.when(g < NG - 1)
        def _():
            x_copy(nxt).wait()
            prepare(nxt)

        second(jnp.maximum(g - 1, 0))
        middle(g)
        first(nxt)
        return 0

    lax.fori_loop(0, NG, main, 0)
    second(NG - 1)

    gt[...] = jnp.transpose(acc[...])
    gb = jnp.sum(gt[E : E + 128, :], axis=0, keepdims=True)
    loss_all = jnp.sum(lacc[...])
    count_all = jnp.sum(counts)
    lane = lax.broadcasted_iota(jnp.int32, (1, 128), 1)
    tail = jnp.where(lane < 64, gb[:, 256:384], jnp.where(lane < 96, loss_all, count_all))
    for j in range(NDP):
        r = j * ROWS
        slot = sb.at[j % NC, j // NC]
        slot[0:ROWS, :] = gt[r : r + ROWS, 0:128]
        slot[ROWS : 2 * ROWS, :] = gt[r : r + ROWS, 128:256]
        half = ROWS // 2
        up = gt[r : r + half, 256:384]
        down = gt[r + half : r + ROWS, 256:384]
        slot[2 * ROWS : 2 * ROWS + half, :] = up + pltpu.roll(down, 64, 1)
        slot[30:31, :] = gb[:, 0:128]
        slot[31:32, :] = gb[:, 128:256]
        slot[32:40, :] = jnp.broadcast_to(tail, (8, 128))

    pair = pltpu.make_async_remote_copy(
        src_ref=sb.at[1 - core], dst_ref=pin, send_sem=c_send, recv_sem=c_recv,
        device_id=(partner, mx), device_id_type=MESH,
    )
    pair.start()
    pair.wait()
    ps[...] = sb[core] + pin[...]
    rr[chip] = ps[chip]

    def r_copy(n):
        return pltpu.make_async_remote_copy(
            src_ref=ps.at[n], dst_ref=rr.at[chip], send_sem=r_send, recv_sem=r_recv,
            device_id=(n * NC + core, mx), device_id_type=MESH,
        )

    for dy, dz in OFFSETS:
        r_copy(chip_at(dy, dz)).start()
    others = rr.at[pl.ds(0, NCHIP - 1)]
    pltpu.make_async_copy(others, others, r_recv).wait()
    mine = jnp.sum(rr[...], axis=0)
    gbl = mine[30:33]
    lane3 = lax.broadcasted_iota(jnp.int32, (3, 128), 1)
    row3 = lax.broadcasted_iota(jnp.int32, (3, 128), 0)
    gbz = jnp.where((row3 < 2) | (lane3 < 64), gbl, 0.0)
    square = jnp.sum(mine[0:30] * mine[0:30]) + jnp.sum(gbz * gbz) * (1.0 / NDP)
    lrow = mine[32:33, :]
    loss_plane = jnp.sum(jnp.where(lane == 64, lrow, 0.0))
    count = jnp.sum(jnp.where(lane == 96, lrow, 0.0))
    lane8 = lax.broadcasted_iota(jnp.int32, (8, 128), 1)
    mine_a = mx * NC + core
    na[mine_a] = jnp.where(lane8 < 64, square, loss_plane)

    def a_copy(dx, c):
        return pltpu.make_async_remote_copy(
            src_ref=na.at[mine_a], dst_ref=na.at[mine_a], send_sem=a_send, recv_sem=a_recv,
            device_id=(chip * NC + c, lax.rem(mx + dx, NX)), device_id_type=MESH,
        )

    for dx in (2, 1, 3):
        for c in range(NC):
            a_copy(dx, c).start()
    a_copy(0, 1 - core).start()
    rest = na.at[pl.ds(0, NX * NC - 1)]
    pltpu.make_async_copy(rest, rest, a_recv).wait()
    line = jnp.sum(na[...], axis=0)
    loss_sum = jnp.sum(jnp.where(lane == 64, line[0:1], 0.0)) * 0.5
    nb[chip] = line

    def b_out(n):
        return pltpu.make_async_remote_copy(
            src_ref=nb.at[chip], dst_ref=nb.at[chip], send_sem=b_send, recv_sem=b_recv,
            device_id=(n * NC + core, mx), device_id_type=MESH,
        )

    for dy, dz in OFFSETS:
        b_out(chip_at(dy, dz)).start()
    rest_b = nb.at[pl.ds(0, NCHIP - 1)]
    pltpu.make_async_copy(rest_b, rest_b, b_recv).wait()
    final = jnp.sum(nb[...], axis=0)
    total = jnp.broadcast_to(final[0:1, 0:1], (1, 128))
    countv = jnp.full((1, 128), count, F32)
    norm = jnp.sqrt(total) / countv
    clip = jnp.minimum(1.0, 1.0 / (norm + 1e-06))
    factor = clip / countv
    clip_o[...] = clip[:, 0:1]
    loss_o[...] = (jnp.full((1, 128), loss_sum, F32) / countv * (1.0 / FULL))[:, 0:1]
    out = mine * factor
    gw_o[:, 0:128] = out[0:ROWS]
    gw_o[:, 128:256] = out[ROWS : 2 * ROWS]
    half = ROWS // 2
    gw_o[0:half, 256:320] = out[2 * ROWS : 2 * ROWS + half, 0:64]
    gw_o[half:ROWS, 256:320] = out[2 * ROWS : 2 * ROWS + half, 64:128]
    gb_o[:, 0:128] = out[30:31]
    gb_o[:, 128:256] = out[31:32]
    gb_o[:, 256:320] = out[32:33, 0:64]

    def drain(g, _):
        for p in (1, 2, 3):
            st_copy(g, p).wait_send()
        return 0

    lax.fori_loop(0, NG, drain, 0)
    sent = ps.at[pl.ds(0, NCHIP - 1)]
    pltpu.make_async_copy(sent, sent, r_send).wait()
    pltpu.make_async_copy(rest, rest, a_send).wait()
    pltpu.make_async_copy(rest_b, rest_b, b_send).wait()


def body(pred_input, proj_weight, proj_bias, targets, block_masks):
    any_spec = pl.BlockSpec(memory_space=pl.ANY)
    vmem_spec = pl.BlockSpec(memory_space=pltpu.VMEM)
    vm = pltpu.VMEM
    dma = pltpu.SemaphoreType.DMA
    loss, clip, gw, gb = pl.pallas_call(
        kernel,
        name="fused",
        out_shape=(
            jax.ShapeDtypeStruct((1, 1), F32),
            jax.ShapeDtypeStruct((1, 1), F32),
            jax.ShapeDtypeStruct((ROWS, FEAT), F32),
            jax.ShapeDtypeStruct((1, FEAT), F32),
        ),
        in_specs=[any_spec] * 5,
        out_specs=(vmem_spec,) * 4,
        scratch_shapes=[
            vm((IMG, PAT, E), BF16),
            vm((IMG, FEAT, PAT), BF16),
            vm((IMG, 4, PAT), jnp.int32),
            vm((ROWS, FEAT), BF16),
            vm((16, FEAT), F32),
            vm((NDP, 16, FEAT), BF16),
            vm((E, FP), F32),
            vm((FEAT, E), BF16),
            vm((1, FEAT), F32),
            vm((FEAT, 128), F32),
            vm((E, NDP * 16), BF16),
            vm((NG, 2 * GI, PAT), F32),
            vm((NX - 1, NG, 2 * GI, PAT), F32),
            vm((IMG, 8, PAT), F32),
            vm((IMG, 8, PAT), F32),
            vm((IMG, 8, PAT), F32),
            vm((FEAT, GI * PAT), F32),
            vm((FEAT, GI * PAT), BF16),
            vm((FP, E + 128), F32),
            vm((8, 128), F32),
            vm((8, PAT), F32),
            vm((E + 128, FP), F32),
            vm((NC, NCHIP, 40, 128), F32),
            vm((NCHIP, 40, 128), F32),
            vm((NCHIP, 40, 128), F32),
            vm((NCHIP, 40, 128), F32),
            vm((NX * NC, 8, 128), F32),
            vm((NCHIP, 8, 128), F32),
            dma((NG,)), dma((NG,)), dma((3,)),
            dma((NX - 1, NG)), dma((NX - 1, NG)),
            dma, dma, dma, dma, dma, dma, dma, dma, dma, dma,
        ],
        compiler_params=pltpu.CompilerParams(
            collective_id=0, has_side_effects=True, vmem_limit_bytes=64 * 1024 * 1024 - 65536,
        ),
    )(
        pred_input,
        proj_weight,
        proj_bias.reshape(1, FEAT),
        jnp.swapaxes(targets, 1, 2),
        block_masks,
    )
    return loss.reshape(()), clip.reshape(()), gw, gb.reshape(FEAT)


def solution(mesh):
    return jax.shard_map(
        body,
        mesh=mesh,
        in_specs=(
            P("dp", None, None), P("dp", "mp"), P("mp"), P("dp", None, "mp"), P("dp", None, None),
        ),
        out_specs=(P(), P(), P("dp", "mp"), P("mp")),
        check_vma=False,
    )
```

time: 170 us -> 63.4 us (0.37)
  Pallas kernels: 0 us -> 55.2 us
  matrix products: 39.6 us -> 0 us
  blocking collectives: 31.7 us -> 0 us
  starting transfers between devices: 28.4 us -> 0 us
  other arithmetic: 27.7 us -> 1.25 us
  local copies, waits for them, and re-layouts: 20.5 us -> 2.59 us
  waiting for transfers between devices: 12.4 us -> 0 us
  between operations: 7.84 us -> 4.14 us
    pallas_call x0 -> x1, Pallas kernels: none -> 55.2 us  [body(): pl.pallas_call(kernel, name='fused', out_shape=(jax.ShapeDtypeStruct((1,...]
    dot_general x2 -> x0, matrix products: 39.6 us -> none  [the longest x1 26.1 us: body(): jnp.dot(inputs_flat, weight_full, preferred_element_type=jnp.float32)]
    psum x4 -> x0, blocking collectives: 31.7 us -> none  [one_axis_at_a_time(): return functools.reduce(lax.psum, axes, value)]
    all_to_all x4 -> x0, starting transfers between devices: 28.4 us -> none  [the longest x3 21.1 us: copy_for_each(): return lax.all_to_all(copies, axis, split_axis=0, concat_axis=0, tiled=True)]
    reshape x3 -> x1, local copies, waits for them, and re-layouts: 16.9 us -> 1.25 us  [body(): proj_bias.reshape(1, FEAT)]
    unnamed x1 -> x0, other arithmetic: 13.8 us -> none
    reduce_sum x8 -> x0, other arithmetic: 12.6 us -> none  [the longest x1 9.94 us: body(): jnp.sum(target_f, axis=1)]
    all_to_all x4 -> x0, waiting for transfers between devices: 12.4 us -> none  [the longest x1 12.2 us: sum_at_owner(): lax.all_to_all(parts, axis, split_axis=0, concat_axis=0, tiled=True)]
  transfers between devices with their start and end apart: 4 -> 0, of which waited for: 2 -> 0; matrix products, arithmetic and copies ran while one was open for 33% -> 0% of each run, Pallas kernels for 0% -> 0%
where the time goes in v1:
time: 63.4 us; the launch traced here: 63.2 us
  Pallas kernels  55.2 us (87%)
  between operations  4.14 us (7%)
  local copies, waits for them, and re-layouts  2.59 us (4%)
  other arithmetic  1.25 us (2%)
    pallas_call x1, Pallas kernels, body(): pl.pallas_call(kernel, name='fused', out_shape=(jax.ShapeDtypeStruct((1,...  55.2 us
    unnamed x1, local copies, waits for them, and re-layouts  1.35 us

profile of v1, /device:TPU:1, one launch (start us, length us, event | category | flops | bytes accessed | tf_op | source)
XLA Modules:
  0.0 63.2 jit_solution(1452972597383045361)
XLA Ops:
  0.6 1.2 %reshape.20.b_hbm = f32[1,320]{1,0:T(1,128)} reshape(f32[320]{0:T(512)} %param.7) | data formatting | bytes 2560 | tf_op jit(solution)/shard_map/reshape | solution.py:419
  1.9 55.2 %fused.1 = (f32[1,1]{1,0:T(1,128)}, f32[1,1]{1,0:T(1,128)}, f32[12,320]{1,0:T(8,128)}, f32[1,320]{1,0:T(1,128)}) custom-call(bf16[64,256,384]{2,1,0:T(8,128)(2,1)} %x_hbm.1, bf16[12,320]{1,0:T(8,128)(2,1)} %w_hbm.1, f32[1,320]{1,0:T(1,128)} %reshape.20.b_hbm, bf16[64,320,256]{2,1,0:T(8,128)(2,1)} %bitcast.3, s32[64,4,256]{2,1,0:T(4,128)} %m_hbm.1), custom_call_target="tpu_custom_call" | custom-call | tf_op jit(solution)/shard_map/fused/pallas_call | solution.py:369
  57.1 1.2 %reduce = f32[320]{0:T(512)} reduce(f32[1,320]{1,0:T(1,128)} %get-tuple-element.11, f32[]{:T(128)} %constant.1), dimensions={0}, to_apply=%get-tuple-element.11.reduce_sub_computation | reduce | bytes 2564 | tf_op jit(solution)/shard_map/fused/pallas_call | solution.py:369
  59.6 1.3 %copy.14 = f32[12,320]{1,0:T(8,128)} copy(f32[12,320]{1,0:T(8,128)} %get-tuple-element.18) | data formatting | bytes 30720

commit v2 on v1

--- a/solution.py
+++ b/solution.py
@@ -24,6 +24,14 @@
 RB = 64
 EARLY = 6
 
+EVERY = sorted(
+    [
+        (dx, dy, dz)
+        for dx in range(NX) for dy in range(NY) for dz in range(NZ)
+        if (dx, dy, dz) != (0, 0, 0)
+    ],
+    key=lambda o: -(min(o[0], NX - o[0]) + min(o[1], NY - o[1]) + min(o[2], NZ - o[2])),
+)
 OFFSETS = sorted(
     [(dy, dz) for dy in range(NY) for dz in range(NZ) if (dy, dz) != (0, 0)],
     key=lambda o: -(min(o[0], NY - o[0]) + min(o[1], NZ - o[1])),
@@ -32,11 +40,11 @@
 
 def kernel(
     x_hbm, w_hbm, b_hbm, t_hbm, m_hbm,
-    loss_o, clip_o, gw_o, gb_o,
-    xv, tv, mv, wi, wtmp, wg, wsq, wt, bi, bias, pm,
-    st_own, st_in, ab, cb, vb, pscr, sscr, acc, gbt, lacc, gt, sb, pin, ps, rr, na, nb,
+    out_o,
+    xv, tv, mv, wi, wtmp, wg, wsq, wt, bi, bias, wide,
+    st_own, st_in, ab, cb, vb, pscr, sscr, acc, lacc, gt, sb, pin, ps, rr, nb,
     x_sem, t_sem, misc_sem,
-    st_send, st_recv, w_send, w_recv, c_send, c_recv, r_send, r_recv, a_send, a_recv, b_send, b_recv,
+    st_send, st_recv, w_send, w_recv, c_send, c_recv, r_send, r_recv, b_send, b_recv,
 ):
     me = lax.axis_index("dp")
     mx = lax.axis_index("mp")
@@ -49,29 +57,6 @@
     def chip_at(dy, dz):
         return lax.rem(my_y + dy, NY) * NZ + lax.rem(my_z + dz, NZ)
 
-    w_copy = pltpu.make_async_copy(w_hbm, wi, misc_sem.at[0])
-    w_copy.start()
-
-    def t_copy(g):
-        return pltpu.make_async_copy(
-            t_hbm.at[pl.ds(g * GI, GI)], tv.at[pl.ds(g * GI, GI)], t_sem.at[g]
-        )
-
-    def x_copy(g):
-        return pltpu.make_async_copy(
-            x_hbm.at[pl.ds(g * GI, GI)], xv.at[pl.ds(g * GI, GI)], x_sem.at[g]
-        )
-
-    def start_t(g, _):
-        t_copy(g).start()
-        return 0
-
-    lax.fori_loop(0, NG, start_t, 0)
-    m_copy = pltpu.make_async_copy(m_hbm, mv, misc_sem.at[1])
-    m_copy.start()
-    b_copy = pltpu.make_async_copy(b_hbm, bi, misc_sem.at[2])
-    b_copy.start()
-
     barrier = pltpu.get_barrier_semaphore()
     for dy, dz in OFFSETS:
         for c in range(NC):
@@ -80,29 +65,52 @@
             )
     pl.semaphore_signal(barrier, inc=1, device_id=(partner, mx), device_id_type=MESH)
     for dx in range(1, NX):
-        for c in range(NC):
-            pl.semaphore_signal(
-                barrier, inc=1,
-                device_id=(chip * NC + c, lax.rem(mx + dx, NX)), device_id_type=MESH,
-            )
+        pl.semaphore_signal(
+            barrier, inc=1, device_id=(me, lax.rem(mx + dx, NX)), device_id_type=MESH
+        )
+
+    w_copy = pltpu.make_async_copy(w_hbm, wi, misc_sem.at[0])
+    w_copy.start()
+    b_copy = pltpu.make_async_copy(b_hbm, bi, misc_sem.at[2])
+    b_copy.start()
+
+    def t_copy(g):
+        return pltpu.make_async_copy(
+            t_hbm.at[pl.ds(g * GI, GI)], tv.at[pl.ds(g * GI, GI)], t_sem.at[g]
+        )
+
+    def x_copy(g):
+        return pltpu.make_async_copy(
+            x_hbm.at[pl.ds(g * GI, GI)], xv.at[pl.ds(g * GI, GI)], x_sem.at[g]
+        )
+
+    def start_t(g, _):
+        t_copy(g).start()
+        return 0
+
+    lax.fori_loop(0, NG, start_t, 0)
+    m_copy = pltpu.make_async_copy(m_hbm, mv, misc_sem.at[1])
+    m_copy.start()
 
     w_copy.wait()
-    wtmp[...] = jnp.zeros_like(wtmp)
-    wtmp[0:ROWS, :] = wi[...].astype(F32)
+    wide[...] = jnp.zeros_like(wide)
+    wf = wi[...].astype(F32)
+    wide[:, 0:FEAT] = wf
+    half = ROWS // 2
+    wtmp[2 * ROWS : 32, :] = jnp.zeros((32 - 2 * ROWS, 128), F32)
+    wtmp[0:ROWS, :] = wide[:, 0:128]
+    wtmp[ROWS : 2 * ROWS, :] = wide[:, 128:256]
+    wtmp[2 * ROWS : 2 * ROWS + half, :] = wide[0:half, 256:384] + pltpu.roll(
+        wide[half:ROWS, 256:384], 64, 1
+    )
     wg[me] = wtmp[...].astype(BF16)
     b_copy.wait()
 
-    row = lax.broadcasted_iota(jnp.int32, (E, NDP * 16), 0)
-    col = lax.broadcasted_iota(jnp.int32, (E, NDP * 16), 1)
-    low = lax.bitwise_and(col, 15)
-    pick = (row == lax.shift_right_logical(col, 4) * ROWS + low) & (low < ROWS)
-    pm[...] = jnp.where(pick, 1.0, 0.0).astype(BF16)
     wsq[...] = jnp.zeros_like(wsq)
-    wsq[0:8, 0:FEAT] = jnp.broadcast_to(bi[...], (8, FEAT))
+    wsq[0:8, 0:FEAT] = jnp.broadcast_to(bi[...].reshape(1, FEAT), (8, FEAT))
     bcol = jnp.transpose(jnp.broadcast_to(wsq[0:1, :], (128, FP)))
     bias[...] = bcol[0:FEAT, :]
     acc[...] = jnp.zeros_like(acc)
-    gbt[...] = jnp.zeros_like(gbt)
     lacc[...] = jnp.zeros_like(lacc)
     sscr[...] = jnp.zeros_like(sscr)
 
@@ -140,7 +148,7 @@
         return 0
 
     lax.fori_loop(0, EARLY, stats_only, 0)
-    pl.semaphore_wait(barrier, (NCHIP - 1) * NC + 1 + (NX - 1) * NC)
+    pl.semaphore_wait(barrier, (NCHIP - 1) * NC + NX)
 
     def w_dst(n):
         return pltpu.make_async_remote_copy(
@@ -196,9 +204,15 @@
     pltpu.make_async_copy(whole, whole, w_recv).wait()
     pltpu.make_async_copy(whole, whole, w_send).wait()
 
-    wsq[:, 0:FEAT] = jnp.dot(
-        pm[...], wg[...].reshape(NDP * 16, FEAT), preferred_element_type=F32
-    )
+    left = lax.broadcasted_iota(jnp.int32, (half, 128), 1) < 64
+    for j in range(NDP):
+        r = j * ROWS
+        wtmp[...] = wg[j].astype(F32)
+        wsq[r : r + ROWS, 0:128] = wtmp[0:ROWS, :]
+        wsq[r : r + ROWS, 128:256] = wtmp[ROWS : 2 * ROWS, :]
+        both = wtmp[2 * ROWS : 2 * ROWS + half, :]
+        wsq[r : r + half, 256:384] = jnp.where(left, both, 0.0)
+        wsq[r + half : r + ROWS, 256:384] = jnp.where(left, pltpu.roll(both, 64, 1), 0.0)
     wt[...] = jnp.transpose(wsq[...])[0:FEAT, :].astype(BF16)
 
     def first(g):
@@ -301,53 +315,34 @@
     lrow = mine[32:33, :]
     loss_plane = jnp.sum(jnp.where(lane == 64, lrow, 0.0))
     count = jnp.sum(jnp.where(lane == 96, lrow, 0.0))
-    lane8 = lax.broadcasted_iota(jnp.int32, (8, 128), 1)
-    mine_a = mx * NC + core
-    na[mine_a] = jnp.where(lane8 < 64, square, loss_plane)
-
-    def a_copy(dx, c):
+    ident = me * NX + mx
+    nb[ident] = jnp.where(lane < 64, square, loss_plane)
+
+    def b_out(n, m):
         return pltpu.make_async_remote_copy(
-            src_ref=na.at[mine_a], dst_ref=na.at[mine_a], send_sem=a_send, recv_sem=a_recv,
-            device_id=(chip * NC + c, lax.rem(mx + dx, NX)), device_id_type=MESH,
-        )
-
-    for dx in (2, 1, 3):
+            src_ref=nb.at[ident], dst_ref=nb.at[ident], send_sem=b_send, recv_sem=b_recv,
+            device_id=(n, m), device_id_type=MESH,
+        )
+
+    for dx, dy, dz in EVERY:
         for c in range(NC):
-            a_copy(dx, c).start()
-    a_copy(0, 1 - core).start()
-    rest = na.at[pl.ds(0, NX * NC - 1)]
-    pltpu.make_async_copy(rest, rest, a_recv).wait()
-    line = jnp.sum(na[...], axis=0)
-    loss_sum = jnp.sum(jnp.where(lane == 64, line[0:1], 0.0)) * 0.5
-    nb[chip] = line
-
-    def b_out(n):
-        return pltpu.make_async_remote_copy(
-            src_ref=nb.at[chip], dst_ref=nb.at[chip], send_sem=b_send, recv_sem=b_recv,
-            device_id=(n * NC + core, mx), device_id_type=MESH,
-        )
-
-    for dy, dz in OFFSETS:
-        b_out(chip_at(dy, dz)).start()
-    rest_b = nb.at[pl.ds(0, NCHIP - 1)]
+            b_out(chip_at(dy, dz) * NC + c, lax.rem(mx + dx, NX)).start()
+    b_out(partner, mx).start()
+    rest_b = nb.at[pl.ds(0, NDP * NX - 1)]
     pltpu.make_async_copy(rest_b, rest_b, b_recv).wait()
-    final = jnp.sum(nb[...], axis=0)
+    parts = [jnp.sum(nb[16 * q : 16 * q + 16], axis=0) for q in range(NDP * NX // 16)]
+    final = ((parts[0] + parts[1]) + (parts[2] + parts[3])) + (
+        (parts[4] + parts[5]) + (parts[6] + parts[7])
+    )
+    loss_sum = jnp.sum(jnp.where(lane == 64, final, 0.0)) * (1.0 / NDP)
     total = jnp.broadcast_to(final[0:1, 0:1], (1, 128))
     countv = jnp.full((1, 128), count, F32)
     norm = jnp.sqrt(total) / countv
     clip = jnp.minimum(1.0, 1.0 / (norm + 1e-06))
     factor = clip / countv
-    clip_o[...] = clip[:, 0:1]
-    loss_o[...] = (jnp.full((1, 128), loss_sum, F32) / countv * (1.0 / FULL))[:, 0:1]
-    out = mine * factor
-    gw_o[:, 0:128] = out[0:ROWS]
-    gw_o[:, 128:256] = out[ROWS : 2 * ROWS]
-    half = ROWS // 2
-    gw_o[0:half, 256:320] = out[2 * ROWS : 2 * ROWS + half, 0:64]
-    gw_o[half:ROWS, 256:320] = out[2 * ROWS : 2 * ROWS + half, 64:128]
-    gb_o[:, 0:128] = out[30:31]
-    gb_o[:, 128:256] = out[31:32]
-    gb_o[:, 256:320] = out[32:33, 0:64]
+    row40 = lax.broadcasted_iota(jnp.int32, (40, 128), 0)
+    loss = jnp.full((1, 128), loss_sum, F32) / countv * (1.0 / FULL)
+    out_o[...] = jnp.where(row40 == 33, loss, jnp.where(row40 == 34, clip, mine * factor))
 
     def drain(g, _):
         for p in (1, 2, 3):
@@ -357,8 +352,20 @@
     lax.fori_loop(0, NG, drain, 0)
     sent = ps.at[pl.ds(0, NCHIP - 1)]
     pltpu.make_async_copy(sent, sent, r_send).wait()
-    pltpu.make_async_copy(rest, rest, a_send).wait()
     pltpu.make_async_copy(rest_b, rest_b, b_send).wait()
+
+
+def spread(in_ref, loss_o, clip_o, gw_o, gb_o):
+    half = ROWS // 2
+    gw_o[:, 0:128] = in_ref[0:ROWS]
+    gw_o[:, 128:256] = in_ref[ROWS : 2 * ROWS]
+    gw_o[0:half, 256:320] = in_ref[2 * ROWS : 2 * ROWS + half, 0:64]
+    gw_o[half:ROWS, 256:320] = in_ref[2 * ROWS : 2 * ROWS + half, 64:128]
+    gb_o[...] = jnp.concatenate(
+        [in_ref[30:31, :], in_ref[31:32, :], in_ref[32:33, 0:64]], axis=1
+    ).reshape(FEAT)
+    loss_o[...] = in_ref[33:34, 0:1]
+    clip_o[...] = in_ref[34:35, 0:1]
 
 
 def body(pred_input, proj_weight, proj_bias, targets, block_masks):
@@ -366,29 +373,24 @@
     vmem_spec = pl.BlockSpec(memory_space=pltpu.VMEM)
     vm = pltpu.VMEM
     dma = pltpu.SemaphoreType.DMA
-    loss, clip, gw, gb = pl.pallas_call(
+    packed = pl.pallas_call(
         kernel,
         name="fused",
-        out_shape=(
-            jax.ShapeDtypeStruct((1, 1), F32),
-            jax.ShapeDtypeStruct((1, 1), F32),
-            jax.ShapeDtypeStruct((ROWS, FEAT), F32),
-            jax.ShapeDtypeStruct((1, FEAT), F32),
-        ),
+        out_shape=jax.ShapeDtypeStruct((40, 128), F32),
         in_specs=[any_spec] * 5,
-        out_specs=(vmem_spec,) * 4,
+        out_specs=vmem_spec,
         scratch_shapes=[
             vm((IMG, PAT, E), BF16),
             vm((IMG, FEAT, PAT), BF16),
             vm((IMG, 4, PAT), jnp.int32),
             vm((ROWS, FEAT), BF16),
-            vm((16, FEAT), F32),
-            vm((NDP, 16, FEAT), BF16),
+            vm((32, 128), F32),
+            vm((NDP, 32, 128), BF16),
             vm((E, FP), F32),
             vm((FEAT, E), BF16),
-            vm((1, FEAT), F32),
+            vm((FEAT,), F32),
             vm((FEAT, 128), F32),
-            vm((E, NDP * 16), BF16),
+            vm((ROWS, FP), F32),
             vm((NG, 2 * GI, PAT), F32),
             vm((NX - 1, NG, 2 * GI, PAT), F32),
             vm((IMG, 8, PAT), F32),
@@ -397,18 +399,16 @@
             vm((FEAT, GI * PAT), F32),
             vm((FEAT, GI * PAT), BF16),
             vm((FP, E + 128), F32),
-            vm((8, 128), F32),
             vm((8, PAT), F32),
             vm((E + 128, FP), F32),
             vm((NC, NCHIP, 40, 128), F32),
             vm((NCHIP, 40, 128), F32),
             vm((NCHIP, 40, 128), F32),
             vm((NCHIP, 40, 128), F32),
-            vm((NX * NC, 8, 128), F32),
-            vm((NCHIP, 8, 128), F32),
+            vm((NDP * NX, 1, 128), F32),
             dma((NG,)), dma((NG,)), dma((3,)),
             dma((NX - 1, NG)), dma((NX - 1, NG)),
-            dma, dma, dma, dma, dma, dma, dma, dma, dma, dma,
+            dma, dma, dma, dma, dma, dma, dma, dma,
         ],
         compiler_params=pltpu.CompilerParams(
             collective_id=0, has_side_effects=True, vmem_limit_bytes=64 * 1024 * 1024 - 65536,
@@ -416,11 +416,23 @@
     )(
         pred_input,
         proj_weight,
-        proj_bias.reshape(1, FEAT),
+        proj_bias,
         jnp.swapaxes(targets, 1, 2),
         block_masks,
     )
-    return loss.reshape(()), clip.reshape(()), gw, gb.reshape(FEAT)
+    loss, clip, gw, gb = pl.pallas_call(
+        spread,
+        name="spread",
+        out_shape=(
+            jax.ShapeDtypeStruct((1, 1), F32),
+            jax.ShapeDtypeStruct((1, 1), F32),
+            jax.ShapeDtypeStruct((ROWS, FEAT), F32),
+            jax.ShapeDtypeStruct((FEAT,), F32),
+        ),
+        in_specs=[vmem_spec],
+        out_specs=(vmem_spec,) * 4,
+    )(packed)
+    return loss.reshape(()), clip.reshape(()), gw, gb
 
 
 def solution(mesh):

time: 63.4 us -> 53.1 us (0.84)
  between operations: 4.14 us -> 0.64 us
  Pallas kernels: 55.2 us -> 52.3 us
  local copies, waits for them, and re-layouts: 2.59 us -> 0 us
  other arithmetic: 1.25 us -> 0 us
    pallas_call x1 -> x2, Pallas kernels: 55.2 us -> 52.3 us  [the longest x1 50.9 us: body(): pl.pallas_call(kernel, name='fused', out_shape=jax.ShapeDtypeStruct((40,...]
    unnamed x1 -> x0, local copies, waits for them, and re-layouts: 1.35 us -> none
    pallas_call x1 -> x0, other arithmetic: 1.25 us -> none  [body(): pl.pallas_call(kernel, name='fused', out_shape=(jax.ShapeDtypeStruct((1,...]
    reshape x1 -> x0, local copies, waits for them, and re-layouts: 1.25 us -> none  [body(): proj_bias.reshape(1, FEAT)]
where the time goes in v2:
time: 53.1 us; the launch traced here: 52.9 us
  Pallas kernels  52.3 us (98%)
  between operations  0.64 us (1%)
    pallas_call x1, Pallas kernels, body(): pl.pallas_call(kernel, name='fused', out_shape=jax.ShapeDtypeStruct((40,...  50.9 us
    pallas_call x1, Pallas kernels, body(): pl.pallas_call(spread, name='spread', out_shape=(jax.ShapeDtypeStruct((1,...  1.41 us

profile of v2, /device:TPU:1, one launch (start us, length us, event | category | flops | bytes accessed | tf_op | source)
XLA Modules:
  0.0 52.9 jit_solution(3166388715437186487)
XLA Ops:
  0.6 50.9 %fused.1.in_ref = f32[40,128]{1,0:T(8,128)} custom-call(bf16[64,256,384]{2,1,0:T(8,128)(2,1)} %x_hbm.1, bf16[12,320]{1,0:T(8,128)(2,1)} %w_hbm.1, f32[320]{0:T(512)} %b_hbm.1, bf16[64,320,256]{2,1,0:T(8,128)(2,1)} %bitcast.3, s32[64,4,256]{2,1,0:T(4,128)} %m_hbm.1), custom_call_target="tpu_custom_call" | custom-call | tf_op jit(solution)/shard_map/fused/pallas_call | solution.py:376
  51.5 1.4 %spread.1 = (f32[1,1]{1,0:T(1,128)}, f32[1,1]{1,0:T(1,128)}, f32[12,320]{1,0:T(8,128)}, f32[320]{0:T(512)}) custom-call(f32[40,128]{1,0:T(8,128)} %fused.1.in_ref), custom_call_target="tpu_custom_call" | custom-call | tf_op jit(solution)/shard_map/spread/pallas_call | solution.py:423

commit v3 on v2

--- a/solution.py
+++ b/solution.py
@@ -22,7 +22,7 @@
 ROWS = E // NDP
 FP = 384
 RB = 64
-EARLY = 6
+XW = 512
 
 EVERY = sorted(
     [
@@ -38,14 +38,24 @@
 )
 
 
-def kernel(
+def kernel(*args):
+    pl.run_scoped(
+        lambda *refs: work(refs[:-2], refs[-2:], *args),
+        *([pltpu.ACC(0)((RB, 256), F32)] * (2 * FEAT // RB) + [pltpu.ACC(1)((FEAT, 256), F32)] * 2),
+    )
+
+
+def work(
+    pieces, grad,
     x_hbm, w_hbm, b_hbm, t_hbm, m_hbm,
     out_o,
-    xv, tv, mv, wi, wtmp, wg, wsq, wt, bi, bias, wide,
-    st_own, st_in, ab, cb, vb, pscr, sscr, acc, lacc, gt, sb, pin, ps, rr, nb,
+    xv, tv, mv, wi, wtmp, wg, wsq, wt, bi, wide,
+    st_own, st_in, ab, cb, vb, sa, sc, acc, lacc, gt, sb, pin, ps, rr, nb,
     x_sem, t_sem, misc_sem,
     st_send, st_recv, w_send, w_recv, c_send, c_recv, r_send, r_recv, b_send, b_recv,
 ):
+    sets = (pieces[: FEAT // RB], pieces[FEAT // RB :])
+    outs = (sa, sc)
     me = lax.axis_index("dp")
     mx = lax.axis_index("mp")
     core = lax.rem(me, NC)
@@ -56,6 +66,11 @@
 
     def chip_at(dy, dz):
         return lax.rem(my_y + dy, NY) * NZ + lax.rem(my_z + dz, NZ)
+
+    w_copy = pltpu.make_async_copy(w_hbm, wi, misc_sem.at[0])
+    w_copy.start()
+    b_copy = pltpu.make_async_copy(b_hbm, bi, misc_sem.at[2])
+    b_copy.start()
 
     barrier = pltpu.get_barrier_semaphore()
     for dy, dz in OFFSETS:
@@ -69,11 +84,6 @@
             barrier, inc=1, device_id=(me, lax.rem(mx + dx, NX)), device_id_type=MESH
         )
 
-    w_copy = pltpu.make_async_copy(w_hbm, wi, misc_sem.at[0])
-    w_copy.start()
-    b_copy = pltpu.make_async_copy(b_hbm, bi, misc_sem.at[2])
-    b_copy.start()
-
     def t_copy(g):
         return pltpu.make_async_copy(
             t_hbm.at[pl.ds(g * GI, GI)], tv.at[pl.ds(g * GI, GI)], t_sem.at[g]
@@ -81,7 +91,7 @@
 
     def x_copy(g):
         return pltpu.make_async_copy(
-            x_hbm.at[pl.ds(g * GI, GI)], xv.at[pl.ds(g * GI, GI)], x_sem.at[g]
+            x_hbm.at[pl.ds(g * GI, GI)], xv.at[pl.ds(g * GI, GI), :, pl.ds(0, E)], x_sem.at[g]
         )
 
     def start_t(g, _):
@@ -104,19 +114,50 @@
         wide[half:ROWS, 256:384], 64, 1
     )
     wg[me] = wtmp[...].astype(BF16)
+
+    pl.semaphore_wait(barrier, (NCHIP - 1) * NC + NX)
+
+    def w_dst(n):
+        return pltpu.make_async_remote_copy(
+            src_ref=wg.at[me],
+            dst_ref=wg.at[me],
+            send_sem=w_send,
+            recv_sem=w_recv,
+            device_id=(n, mx),
+            device_id_type=MESH,
+        )
+
+    for dy, dz in OFFSETS:
+        for c in range(NC):
+            w_dst(chip_at(dy, dz) * NC + c).start()
+    w_dst(partner).start()
+
     b_copy.wait()
-
     wsq[...] = jnp.zeros_like(wsq)
-    wsq[0:8, 0:FEAT] = jnp.broadcast_to(bi[...].reshape(1, FEAT), (8, FEAT))
-    bcol = jnp.transpose(jnp.broadcast_to(wsq[0:1, :], (128, FP)))
-    bias[...] = bcol[0:FEAT, :]
+    b_all = bi[...].reshape(1, FEAT)
+    b_high = b_all.astype(BF16).astype(F32)
+    b_mid = (b_all - b_high).astype(BF16).astype(F32)
+    wsq[E : E + 1, 0:FEAT] = b_high
+    wsq[E + 1 : E + 2, 0:FEAT] = b_mid
+    wsq[E + 2 : E + 3, 0:FEAT] = (b_all - b_high) - b_mid
     acc[...] = jnp.zeros_like(acc)
     lacc[...] = jnp.zeros_like(lacc)
-    sscr[...] = jnp.zeros_like(sscr)
+    sc[...] = jnp.zeros_like(sc)
+    none = jnp.zeros((RB, 256), BF16)
+    for q in range(2):
+        pltpu.matmul_acc_lhs(pieces[0], none, load_staged_rhs=q)
+        pltpu.matmul_acc_lhs(grad[0], jnp.zeros((FEAT, 256), BF16), load_staged_rhs=q)
+    for piece in (*pieces, *grad):
+        pltpu.matmul_pop(piece)
+
+
+    lane_x = lax.broadcasted_iota(jnp.int32, (1, 1, XW - E), 2)
+    ones = jnp.where(lane_x < 3, 1.0, 0.0).astype(BF16)
 
     def stats(g):
         t_copy(g).wait()
         x_copy(g).start()
+        xv[pl.ds(g * GI, GI), :, E:XW] = jnp.broadcast_to(ones, (GI, PAT, XW - E))
         sums, squares = [], []
         for k in range(GI):
             s8 = jnp.zeros((8, PAT), F32)
@@ -143,40 +184,14 @@
         for p in (2, 1, 3):
             st_copy(g, p).start()
 
-    def stats_only(g, _):
-        stats(g)
-        return 0
-
-    lax.fori_loop(0, EARLY, stats_only, 0)
-    pl.semaphore_wait(barrier, (NCHIP - 1) * NC + NX)
-
-    def w_dst(n):
-        return pltpu.make_async_remote_copy(
-            src_ref=wg.at[me],
-            dst_ref=wg.at[me],
-            send_sem=w_send,
-            recv_sem=w_recv,
-            device_id=(n, mx),
-            device_id_type=MESH,
-        )
-
-    for dy, dz in OFFSETS:
-        for c in range(NC):
-            w_dst(chip_at(dy, dz) * NC + c).start()
-    w_dst(partner).start()
-
-    def send_early(g, _):
-        send_stats(g)
-        return 0
-
-    lax.fori_loop(0, EARLY - 1, send_early, 0)
+    stats(0)
 
     def stats_and_send(g, _):
         stats(g)
         send_stats(g - 1)
         return 0
 
-    lax.fori_loop(EARLY, NG, stats_and_send, 0)
+    lax.fori_loop(1, NG, stats_and_send, 0)
 
     m_copy.wait()
 
@@ -202,7 +217,6 @@
 
     whole = wg.at[pl.ds(0, NDP - 1)]
     pltpu.make_async_copy(whole, whole, w_recv).wait()
-    pltpu.make_async_copy(whole, whole, w_send).wait()
 
     left = lax.broadcasted_iota(jnp.int32, (half, 128), 1) < 64
     for j in range(NDP):
@@ -215,58 +229,69 @@
         wsq[r + half : r + ROWS, 256:384] = jnp.where(left, pltpu.roll(both, 64, 1), 0.0)
     wt[...] = jnp.transpose(wsq[...])[0:FEAT, :].astype(BF16)
 
-    def first(g):
-        for k in range(GI):
-            pscr[:, k * PAT : (k + 1) * PAT] = lax.dot_general(
-                wt[...], xv[g * GI + k], (((1,), (1,)), ((), ())), preferred_element_type=F32
+    def first(i, pieces):
+        for q in range(2):
+            pltpu.matmul_push_rhs(
+                xv[i, :, 256 * q : 256 * q + 256], staging_register=q, mxu_index=0, transpose=True
             )
-
-    def second(g):
-        xs = xv[pl.ds(g * GI, GI)].reshape(GI * PAT, E)
-        acc[0:FEAT, 0:E] += jnp.dot(sscr[...], xs, preferred_element_type=F32)
-
-    def middle(g):
+        for q in range(2):
+            for n, piece in enumerate(pieces):
+                pltpu.matmul_acc_lhs(
+                    piece, wt[RB * n : RB * n + RB, 256 * q : 256 * q + 256],
+                    load_staged_rhs=q if n == 0 else None,
+                )
+
+    def second(i, source):
+        for q in range(2):
+            pltpu.matmul_push_rhs(
+                xv[i, :, 256 * q : 256 * q + 256], staging_register=q, mxu_index=1
+            )
+        for q in range(2):
+            pltpu.matmul_acc_lhs(grad[q], source[...], load_staged_rhs=q)
+
+    def middle(i, pieces, target):
+        a = ab[i][None]
+        c = cb[i][None]
+        v = vb[i][None]
         loss8 = jnp.zeros((8, PAT), F32)
-        for r in range(0, FEAT, RB):
-            bb = bias[r : r + RB, :]
-            b2 = jnp.concatenate([bb, bb], axis=1).reshape(RB // 8, 8, PAT)
-            gsum = jnp.zeros((RB // 8, 8, PAT), F32)
-            for k in range(GI):
-                i = g * GI + k
-                a = ab[i][None]
-                c = cb[i][None]
-                v = vb[i][None]
-                p = pscr[r : r + RB, k * PAT : (k + 1) * PAT].reshape(RB // 8, 8, PAT)
-                t = tv[i, r : r + RB, :].astype(F32).reshape(RB // 8, 8, PAT)
-                d = (p + b2) - (t * a - c)
-                h = jnp.minimum(jnp.maximum(d, -1.0), 1.0)
-                s = v * h
-                loss8 = loss8 + jnp.sum(s * (d - 0.5 * h), axis=0)
-                gsum = gsum + s
-                sscr[r : r + RB, k * PAT : (k + 1) * PAT] = s.reshape(RB, PAT).astype(BF16)
-            gs = gsum.reshape(RB, PAT)
-            acc[r : r + RB, E : E + 128] += gs[:, 0:128] + gs[:, 128:256]
+        for n, piece in enumerate(pieces):
+            r = RB * n
+            p = pltpu.matmul_pop(piece).reshape(RB // 8, 8, PAT)
+            t = tv[i, r : r + RB, :].astype(F32).reshape(RB // 8, 8, PAT)
+            d = p - (t * a - c)
+            h = jnp.minimum(jnp.maximum(d, -1.0), 1.0)
+            s = v * h
+            loss8 = loss8 + jnp.sum(s * (d - 0.5 * h), axis=0)
+            s = s.reshape(RB, PAT)
+            target[r : r + RB, :] = s.astype(BF16)
+            acc[r : r + RB, E : E + 128] += s[:, 0:128] + s[:, 128:256]
         lacc[...] += loss8
 
     x_copy(0).wait()
-    first(0)
+    first(0, sets[0])
     prepare(0)
 
     def main(g, _):
         nxt = jnp.minimum(g + 1, NG - 1)
 
-        @pl.when(g < NG - 1)
+        @pl.when(g + 1 < NG)
         def _():
             x_copy(nxt).wait()
             prepare(nxt)
 
-        second(jnp.maximum(g - 1, 0))
-        middle(g)
-        first(nxt)
+        base = g * GI
+        for u in range(GI):
+            first(jnp.minimum(base + u + 1, IMG - 1), sets[(u + 1) % 2])
+            second(jnp.maximum(base + u - 1, 0), outs[(u + 1) % 2])
+            middle(base + u, sets[u % 2], outs[u % 2])
         return 0
 
     lax.fori_loop(0, NG, main, 0)
-    second(NG - 1)
+    second(IMG - 1, outs[1])
+    acc[0:FEAT, 0:256] = pltpu.matmul_pop(grad[0])
+    acc[0:FEAT, 256:E] = pltpu.matmul_pop(grad[1])[:, 0:128]
+    for piece in sets[0]:
+        pltpu.matmul_pop(piece)
 
     gt[...] = jnp.transpose(acc[...])
     gb = jnp.sum(gt[E : E + 128, :], axis=0, keepdims=True)
@@ -350,6 +375,7 @@
         return 0
 
     lax.fori_loop(0, NG, drain, 0)
+    pltpu.make_async_copy(whole, whole, w_send).wait()
     sent = ps.at[pl.ds(0, NCHIP - 1)]
     pltpu.make_async_copy(sent, sent, r_send).wait()
     pltpu.make_async_copy(rest_b, rest_b, b_send).wait()
@@ -380,24 +406,23 @@
         in_specs=[any_spec] * 5,
         out_specs=vmem_spec,
         scratch_shapes=[
-            vm((IMG, PAT, E), BF16),
+            vm((IMG, PAT, XW), BF16),
             vm((IMG, FEAT, PAT), BF16),
             vm((IMG, 4, PAT), jnp.int32),
             vm((ROWS, FEAT), BF16),
             vm((32, 128), F32),
             vm((NDP, 32, 128), BF16),
-            vm((E, FP), F32),
-            vm((FEAT, E), BF16),
+            vm((XW, FP), F32),
+            vm((FEAT, XW), BF16),
             vm((FEAT,), F32),
-            vm((FEAT, 128), F32),
             vm((ROWS, FP), F32),
             vm((NG, 2 * GI, PAT), F32),
             vm((NX - 1, NG, 2 * GI, PAT), F32),
             vm((IMG, 8, PAT), F32),
             vm((IMG, 8, PAT), F32),
             vm((IMG, 8, PAT), F32),
-            vm((FEAT, GI * PAT), F32),
-            vm((FEAT, GI * PAT), BF16),
+            vm((FEAT, PAT), BF16),
+            vm((FEAT, PAT), BF16),
             vm((FP, E + 128), F32),
             vm((8, PAT), F32),
             vm((E + 128, FP), F32),

time: 53.1 us -> 48.1 us (0.906)
  Pallas kernels: 52.3 us -> 47.2 us
    pallas_call x1, Pallas kernels: 50.9 us -> 45.8 us  [body(): pl.pallas_call(kernel, name='fused', out_shape=jax.ShapeDtypeStruct((40,...]
where the time goes in v3:
time: 48.1 us; the launch traced here: 47.9 us
  Pallas kernels  47.2 us (98%)
  between operations  0.64 us (1%)
    pallas_call x1, Pallas kernels, body(): pl.pallas_call(kernel, name='fused', out_shape=jax.ShapeDtypeStruct((40,...  45.8 us
    pallas_call x1, Pallas kernels, body(): pl.pallas_call(spread, name='spread', out_shape=(jax.ShapeDtypeStruct((1,...  1.41 us

profile of v3, /device:TPU:1, one launch (start us, length us, event | category | flops | bytes accessed | tf_op | source)
XLA Modules:
  0.0 47.9 jit_solution(1076747936582895588)
XLA Ops:
  0.6 45.8 %fused.1.in_ref = f32[40,128]{1,0:T(8,128)} custom-call(bf16[64,256,384]{2,1,0:T(8,128)(2,1)} %args_0_.4, bf16[12,320]{1,0:T(8,128)(2,1)} %args_1_.4, f32[320]{0:T(512)} %args_2_.4, bf16[64,320,256]{2,1,0:T(8,128)(2,1)} %bitcast.3, s32[64,4,256]{2,1,0:T(4,128)} %args_4_.4), custom_call_target="tpu_custom_call" | custom-call | tf_op jit(solution)/shard_map/fused/pallas_call | solution.py:402
  46.5 1.4 %spread.1 = (f32[1,1]{1,0:T(1,128)}, f32[1,1]{1,0:T(1,128)}, f32[12,320]{1,0:T(8,128)}, f32[320]{0:T(512)}) custom-call(f32[40,128]{1,0:T(8,128)} %fused.1.in_ref), custom_call_target="tpu_custom_call" | custom-call | tf_op jit(solution)/shard_map/spread/pallas_call | solution.py:448

commit v4 on v3

--- a/solution.py
+++ b/solution.py
@@ -23,6 +23,8 @@
 FP = 384
 RB = 64
 XW = 512
+UNROLL = 8
+SLOT = 33
 
 EVERY = sorted(
     [
@@ -52,7 +54,7 @@
     xv, tv, mv, wi, wtmp, wg, wsq, wt, bi, wide,
     st_own, st_in, ab, cb, vb, sa, sc, acc, lacc, gt, sb, pin, ps, rr, nb,
     x_sem, t_sem, misc_sem,
-    st_send, st_recv, w_send, w_recv, c_send, c_recv, r_send, r_recv, b_send, b_recv,
+    st_send, st_recv, w_send, w_recv, wp_send, wp_recv, c_send, c_recv, r_send, r_recv, b_send, b_recv,
 ):
     sets = (pieces[: FEAT // RB], pieces[FEAT // RB :])
     outs = (sa, sc)
@@ -113,24 +115,22 @@
     wtmp[2 * ROWS : 2 * ROWS + half, :] = wide[0:half, 256:384] + pltpu.roll(
         wide[half:ROWS, 256:384], 64, 1
     )
-    wg[me] = wtmp[...].astype(BF16)
+    wg[core, chip] = wtmp[...].astype(BF16)
 
     pl.semaphore_wait(barrier, (NCHIP - 1) * NC + NX)
 
     def w_dst(n):
         return pltpu.make_async_remote_copy(
-            src_ref=wg.at[me],
-            dst_ref=wg.at[me],
+            src_ref=wg.at[core, chip],
+            dst_ref=wg.at[core, chip],
             send_sem=w_send,
             recv_sem=w_recv,
-            device_id=(n, mx),
+            device_id=(n * NC + core, mx),
             device_id_type=MESH,
         )
 
     for dy, dz in OFFSETS:
-        for c in range(NC):
-            w_dst(chip_at(dy, dz) * NC + c).start()
-    w_dst(partner).start()
+        w_dst(chip_at(dy, dz)).start()
 
     b_copy.wait()
     wsq[...] = jnp.zeros_like(wsq)
@@ -215,13 +215,25 @@
             ab[g * GI + k] = jnp.broadcast_to(a[k : k + 1], (8, PAT))
             cb[g * GI + k] = jnp.broadcast_to(c[k : k + 1], (8, PAT))
 
-    whole = wg.at[pl.ds(0, NDP - 1)]
+    def prepare_all(g, _):
+        prepare(g)
+        return 0
+
+    lax.fori_loop(0, NG // 4, prepare_all, 0)
+
+    whole = wg.at[0, pl.ds(0, NCHIP - 1)]
     pltpu.make_async_copy(whole, whole, w_recv).wait()
+    w_pair = pltpu.make_async_remote_copy(
+        src_ref=wg.at[core], dst_ref=wg.at[core], send_sem=wp_send, recv_sem=wp_recv,
+        device_id=(partner, mx), device_id_type=MESH,
+    )
+    w_pair.start()
+    w_pair.wait_recv()
 
     left = lax.broadcasted_iota(jnp.int32, (half, 128), 1) < 64
     for j in range(NDP):
         r = j * ROWS
-        wtmp[...] = wg[j].astype(F32)
+        wtmp[...] = wg[j % NC, j // NC].astype(F32)
         wsq[r : r + ROWS, 0:128] = wtmp[0:ROWS, :]
         wsq[r : r + ROWS, 128:256] = wtmp[ROWS : 2 * ROWS, :]
         both = wtmp[2 * ROWS : 2 * ROWS + half, :]
@@ -267,26 +279,25 @@
             acc[r : r + RB, E : E + 128] += s[:, 0:128] + s[:, 128:256]
         lacc[...] += loss8
 
-    x_copy(0).wait()
+    def x_here(g, _):
+        x_copy(g).wait()
+        return 0
+
+    lax.fori_loop(0, NG, x_here, 0)
     first(0, sets[0])
-    prepare(0)
 
     def main(g, _):
-        nxt = jnp.minimum(g + 1, NG - 1)
-
-        @pl.when(g + 1 < NG)
-        def _():
-            x_copy(nxt).wait()
-            prepare(nxt)
-
-        base = g * GI
-        for u in range(GI):
+        base = g * UNROLL
+        for u in range(UNROLL):
             first(jnp.minimum(base + u + 1, IMG - 1), sets[(u + 1) % 2])
             second(jnp.maximum(base + u - 1, 0), outs[(u + 1) % 2])
             middle(base + u, sets[u % 2], outs[u % 2])
         return 0
 
-    lax.fori_loop(0, NG, main, 0)
+    trips = IMG // UNROLL
+    lax.fori_loop(0, trips // 4, main, 0)
+    lax.fori_loop(NG // 4, NG, prepare_all, 0)
+    lax.fori_loop(trips // 4, trips, main, 0)
     second(IMG - 1, outs[1])
     acc[0:FEAT, 0:256] = pltpu.matmul_pop(grad[0])
     acc[0:FEAT, 256:E] = pltpu.matmul_pop(grad[1])[:, 0:128]
@@ -310,28 +321,40 @@
         slot[2 * ROWS : 2 * ROWS + half, :] = up + pltpu.roll(down, 64, 1)
         slot[30:31, :] = gb[:, 0:128]
         slot[31:32, :] = gb[:, 128:256]
-        slot[32:40, :] = jnp.broadcast_to(tail, (8, 128))
-
-    pair = pltpu.make_async_remote_copy(
-        src_ref=sb.at[1 - core], dst_ref=pin, send_sem=c_send, recv_sem=c_recv,
-        device_id=(partner, mx), device_id_type=MESH,
-    )
-    pair.start()
-    pair.wait()
-    ps[...] = sb[core] + pin[...]
-    rr[chip] = ps[chip]
+        slot[32:33, :] = tail
+
+    order = [chip_at(dy, dz) for dy, dz in OFFSETS] + [chip]
+
+    def pair(k):
+        n = order[k]
+        return pltpu.make_async_remote_copy(
+            src_ref=sb.at[1 - core, n, pl.ds(0, SLOT)], dst_ref=pin.at[n, pl.ds(0, SLOT)],
+            send_sem=c_send.at[k], recv_sem=c_recv.at[k],
+            device_id=(partner, mx), device_id_type=MESH,
+        )
 
     def r_copy(n):
         return pltpu.make_async_remote_copy(
-            src_ref=ps.at[n], dst_ref=rr.at[chip], send_sem=r_send, recv_sem=r_recv,
+            src_ref=ps.at[n, pl.ds(0, SLOT)], dst_ref=rr.at[chip, pl.ds(0, SLOT)],
+            send_sem=r_send, recv_sem=r_recv,
             device_id=(n * NC + core, mx), device_id_type=MESH,
         )
 
-    for dy, dz in OFFSETS:
-        r_copy(chip_at(dy, dz)).start()
-    others = rr.at[pl.ds(0, NCHIP - 1)]
+    for k in range(NCHIP):
+        pair(k).start()
+    for k in range(NCHIP):
+        n = order[k]
+        pair(k).wait_recv()
+        both = sb[core, n, 0:SLOT] + pin[n, 0:SLOT]
+        if k < NCHIP - 1:
+            ps[n, 0:SLOT] = both
+        else:
+            rr[n, 0:SLOT] = both
+        if k > 0:
+            r_copy(order[k - 1]).start()
+    others = rr.at[pl.ds(0, NCHIP - 1), pl.ds(0, SLOT)]
     pltpu.make_async_copy(others, others, r_recv).wait()
-    mine = jnp.sum(rr[...], axis=0)
+    mine = jnp.sum(rr[:, 0:SLOT], axis=0)
     gbl = mine[30:33]
     lane3 = lax.broadcasted_iota(jnp.int32, (3, 128), 1)
     row3 = lax.broadcasted_iota(jnp.int32, (3, 128), 0)
@@ -365,9 +388,11 @@
     norm = jnp.sqrt(total) / countv
     clip = jnp.minimum(1.0, 1.0 / (norm + 1e-06))
     factor = clip / countv
-    row40 = lax.broadcasted_iota(jnp.int32, (40, 128), 0)
     loss = jnp.full((1, 128), loss_sum, F32) / countv * (1.0 / FULL)
-    out_o[...] = jnp.where(row40 == 33, loss, jnp.where(row40 == 34, clip, mine * factor))
+    out_o[0:SLOT] = mine * factor
+    out_o[SLOT : SLOT + 1] = loss
+    out_o[SLOT + 1 : SLOT + 2] = clip
+    out_o[SLOT + 2 :] = jnp.zeros((40 - SLOT - 2, 128), F32)
 
     def drain(g, _):
         for p in (1, 2, 3):
@@ -376,7 +401,10 @@
 
     lax.fori_loop(0, NG, drain, 0)
     pltpu.make_async_copy(whole, whole, w_send).wait()
-    sent = ps.at[pl.ds(0, NCHIP - 1)]
+    w_pair.wait_send()
+    for k in range(NCHIP):
+        pair(k).wait_send()
+    sent = ps.at[pl.ds(0, NCHIP - 1), pl.ds(0, SLOT)]
     pltpu.make_async_copy(sent, sent, r_send).wait()
     pltpu.make_async_copy(rest_b, rest_b, b_send).wait()
 
@@ -411,7 +439,7 @@
             vm((IMG, 4, PAT), jnp.int32),
             vm((ROWS, FEAT), BF16),
             vm((32, 128), F32),
-            vm((NDP, 32, 128), BF16),
+            vm((NC, NCHIP, 32, 128), BF16),
             vm((XW, FP), F32),
             vm((FEAT, XW), BF16),
             vm((FEAT,), F32),
@@ -433,7 +461,7 @@
             vm((NDP * NX, 1, 128), F32),
             dma((NG,)), dma((NG,)), dma((3,)),
             dma((NX - 1, NG)), dma((NX - 1, NG)),
-            dma, dma, dma, dma, dma, dma, dma, dma,
+            dma, dma, dma, dma, dma((NCHIP,)), dma((NCHIP,)), dma, dma, dma, dma,
         ],
         compiler_params=pltpu.CompilerParams(
             collective_id=0, has_side_effects=True, vmem_limit_bytes=64 * 1024 * 1024 - 65536,

time: 48.1 us -> 45.4 us (0.944)
  Pallas kernels: 47.2 us -> 44.6 us
    pallas_call x1, Pallas kernels: 45.8 us -> 43.2 us  [body(): pl.pallas_call(kernel, name='fused', out_shape=jax.ShapeDtypeStruct((40,...]
where the time goes in v4:
time: 45.4 us; the launch traced here: 45.2 us
  Pallas kernels  44.6 us (98%)
  between operations  0.64 us (1%)
    pallas_call x1, Pallas kernels, body(): pl.pallas_call(kernel, name='fused', out_shape=jax.ShapeDtypeStruct((40,...  43.2 us
    pallas_call x1, Pallas kernels, body(): pl.pallas_call(spread, name='spread', out_shape=(jax.ShapeDtypeStruct((1,...  1.41 us

profile of v4, /device:TPU:1, one launch (start us, length us, event | category | flops | bytes accessed | tf_op | source)
XLA Modules:
  0.0 45.2 jit_solution(11508775966597486218)
XLA Ops:
  0.6 43.2 %fused.1.in_ref = f32[40,128]{1,0:T(8,128)} custom-call(bf16[64,256,384]{2,1,0:T(8,128)(2,1)} %args_0_.4, bf16[12,320]{1,0:T(8,128)(2,1)} %args_1_.4, f32[320]{0:T(512)} %args_2_.4, bf16[64,320,256]{2,1,0:T(8,128)(2,1)} %bitcast.3, s32[64,4,256]{2,1,0:T(4,128)} %args_4_.4), custom_call_target="tpu_custom_call" | custom-call | tf_op jit(solution)/shard_map/fused/pallas_call | solution.py:430
  43.8 1.4 %spread.1 = (f32[1,1]{1,0:T(1,128)}, f32[1,1]{1,0:T(1,128)}, f32[12,320]{1,0:T(8,128)}, f32[320]{0:T(512)}) custom-call(f32[40,128]{1,0:T(8,128)} %fused.1.in_ref), custom_call_target="tpu_custom_call" | custom-call | tf_op jit(solution)/shard_map/spread/pallas_call | solution.py:476

commit v5 on v4

--- a/solution.py
+++ b/solution.py
@@ -23,7 +23,7 @@
 FP = 384
 RB = 64
 XW = 512
-UNROLL = 8
+UNROLL = 16
 SLOT = 33
 
 EVERY = sorted(
@@ -51,7 +51,7 @@
     pieces, grad,
     x_hbm, w_hbm, b_hbm, t_hbm, m_hbm,
     out_o,
-    xv, tv, mv, wi, wtmp, wg, wsq, wt, bi, wide,
+    xv, tv, mv, wi, wtmp, wf32, wg, wsq, wt, bi, wide,
     st_own, st_in, ab, cb, vb, sa, sc, acc, lacc, gt, sb, pin, ps, rr, nb,
     x_sem, t_sem, misc_sem,
     st_send, st_recv, w_send, w_recv, wp_send, wp_recv, c_send, c_recv, r_send, r_recv, b_send, b_recv,
@@ -215,12 +215,6 @@
             ab[g * GI + k] = jnp.broadcast_to(a[k : k + 1], (8, PAT))
             cb[g * GI + k] = jnp.broadcast_to(c[k : k + 1], (8, PAT))
 
-    def prepare_all(g, _):
-        prepare(g)
-        return 0
-
-    lax.fori_loop(0, NG // 4, prepare_all, 0)
-
     whole = wg.at[0, pl.ds(0, NCHIP - 1)]
     pltpu.make_async_copy(whole, whole, w_recv).wait()
     w_pair = pltpu.make_async_remote_copy(
@@ -228,15 +222,22 @@
         device_id=(partner, mx), device_id_type=MESH,
     )
     w_pair.start()
+
+    def prepare_all(g, _):
+        prepare(g)
+        return 0
+
+    lax.fori_loop(0, NG // 4, prepare_all, 0)
+
     w_pair.wait_recv()
 
     left = lax.broadcasted_iota(jnp.int32, (half, 128), 1) < 64
     for j in range(NDP):
         r = j * ROWS
-        wtmp[...] = wg[j % NC, j // NC].astype(F32)
-        wsq[r : r + ROWS, 0:128] = wtmp[0:ROWS, :]
-        wsq[r : r + ROWS, 128:256] = wtmp[ROWS : 2 * ROWS, :]
-        both = wtmp[2 * ROWS : 2 * ROWS + half, :]
+        wf32[j] = wg[j % NC, j // NC].astype(F32)
+        wsq[r : r + ROWS, 0:128] = wf32[j, 0:ROWS]
+        wsq[r : r + ROWS, 128:256] = wf32[j, ROWS : 2 * ROWS]
+        both = wf32[j, 2 * ROWS : 2 * ROWS + half]
         wsq[r : r + half, 256:384] = jnp.where(left, both, 0.0)
         wsq[r + half : r + ROWS, 256:384] = jnp.where(left, pltpu.roll(both, 64, 1), 0.0)
     wt[...] = jnp.transpose(wsq[...])[0:FEAT, :].astype(BF16)
@@ -359,12 +360,13 @@
     lane3 = lax.broadcasted_iota(jnp.int32, (3, 128), 1)
     row3 = lax.broadcasted_iota(jnp.int32, (3, 128), 0)
     gbz = jnp.where((row3 < 2) | (lane3 < 64), gbl, 0.0)
-    square = jnp.sum(mine[0:30] * mine[0:30]) + jnp.sum(gbz * gbz) * (1.0 / NDP)
+    squares = jnp.sum(mine[0:30] * mine[0:30], axis=0, keepdims=True) + jnp.sum(
+        gbz * gbz, axis=0, keepdims=True
+    ) * (1.0 / NDP)
     lrow = mine[32:33, :]
-    loss_plane = jnp.sum(jnp.where(lane == 64, lrow, 0.0))
-    count = jnp.sum(jnp.where(lane == 96, lrow, 0.0))
     ident = me * NX + mx
-    nb[ident] = jnp.where(lane < 64, square, loss_plane)
+    nb[ident, 0:1] = squares
+    nb[ident, 1:2] = lrow
 
     def b_out(n, m):
         return pltpu.make_async_remote_copy(
@@ -377,13 +379,26 @@
             b_out(chip_at(dy, dz) * NC + c, lax.rem(mx + dx, NX)).start()
     b_out(partner, mx).start()
     rest_b = nb.at[pl.ds(0, NDP * NX - 1)]
+    def drain(g, _):
+        for p in (1, 2, 3):
+            st_copy(g, p).wait_send()
+        return 0
+
+    lax.fori_loop(0, NG, drain, 0)
+    pltpu.make_async_copy(whole, whole, w_send).wait()
+    w_pair.wait_send()
+    for k in range(NCHIP):
+        pair(k).wait_send()
+    sent = ps.at[pl.ds(0, NCHIP - 1), pl.ds(0, SLOT)]
+    pltpu.make_async_copy(sent, sent, r_send).wait()
     pltpu.make_async_copy(rest_b, rest_b, b_recv).wait()
     parts = [jnp.sum(nb[16 * q : 16 * q + 16], axis=0) for q in range(NDP * NX // 16)]
     final = ((parts[0] + parts[1]) + (parts[2] + parts[3])) + (
         (parts[4] + parts[5]) + (parts[6] + parts[7])
     )
-    loss_sum = jnp.sum(jnp.where(lane == 64, final, 0.0)) * (1.0 / NDP)
-    total = jnp.broadcast_to(final[0:1, 0:1], (1, 128))
+    loss_sum = jnp.sum(jnp.where(lane == 64, final[1:2], 0.0)) * (1.0 / NDP)
+    count = jnp.sum(jnp.where(lane == 96, lrow, 0.0))
+    total = jnp.full((1, 128), jnp.sum(final[0:1]), F32)
     countv = jnp.full((1, 128), count, F32)
     norm = jnp.sqrt(total) / countv
     clip = jnp.minimum(1.0, 1.0 / (norm + 1e-06))
@@ -393,19 +408,6 @@
     out_o[SLOT : SLOT + 1] = loss
     out_o[SLOT + 1 : SLOT + 2] = clip
     out_o[SLOT + 2 :] = jnp.zeros((40 - SLOT - 2, 128), F32)
-
-    def drain(g, _):
-        for p in (1, 2, 3):
-            st_copy(g, p).wait_send()
-        return 0
-
-    lax.fori_loop(0, NG, drain, 0)
-    pltpu.make_async_copy(whole, whole, w_send).wait()
-    w_pair.wait_send()
-    for k in range(NCHIP):
-        pair(k).wait_send()
-    sent = ps.at[pl.ds(0, NCHIP - 1), pl.ds(0, SLOT)]
-    pltpu.make_async_copy(sent, sent, r_send).wait()
     pltpu.make_async_copy(rest_b, rest_b, b_send).wait()
 
 
@@ -439,6 +441,7 @@
             vm((IMG, 4, PAT), jnp.int32),
             vm((ROWS, FEAT), BF16),
             vm((32, 128), F32),
+            vm((NDP, 32, 128), F32),
             vm((NC, NCHIP, 32, 128), BF16),
             vm((XW, FP), F32),
             vm((FEAT, XW), BF16),
@@ -458,7 +461,7 @@
             vm((NCHIP, 40, 128), F32),
             vm((NCHIP, 40, 128), F32),
             vm((NCHIP, 40, 128), F32),
-            vm((NDP * NX, 1, 128), F32),
+            vm((NDP * NX, 2, 128), F32),
             dma((NG,)), dma((NG,)), dma((3,)),
             dma((NX - 1, NG)), dma((NX - 1, NG)),
             dma, dma, dma, dma, dma((NCHIP,)), dma((NCHIP,)), dma, dma, dma, dma,

time: 45.4 us -> 44.7 us (0.985)
  Pallas kernels: 44.6 us -> 43.9 us
    pallas_call x1, Pallas kernels: 43.2 us -> 42.5 us  [body(): pl.pallas_call(kernel, name='fused', out_shape=jax.ShapeDtypeStruct((40,...]
where the time goes in v5:
time: 44.7 us; the launch traced here: 44.5 us
  Pallas kernels  43.9 us (98%)
  between operations  0.64 us (1%)
    pallas_call x1, Pallas kernels, body(): pl.pallas_call(kernel, name='fused', out_shape=jax.ShapeDtypeStruct((40,...  42.5 us
    pallas_call x1, Pallas kernels, body(): pl.pallas_call(spread, name='spread', out_shape=(jax.ShapeDtypeStruct((1,...  1.41 us

profile of v5, /device:TPU:1, one launch (start us, length us, event | category | flops | bytes accessed | tf_op | source)
XLA Modules:
  0.0 44.5 jit_solution(11734723092838752592)
XLA Ops:
  0.6 42.5 %fused.1.in_ref = f32[40,128]{1,0:T(8,128)} custom-call(bf16[64,256,384]{2,1,0:T(8,128)(2,1)} %args_0_.4, bf16[12,320]{1,0:T(8,128)(2,1)} %args_1_.4, f32[320]{0:T(512)} %args_2_.4, bf16[64,320,256]{2,1,0:T(8,128)(2,1)} %bitcast.3, s32[64,4,256]{2,1,0:T(4,128)} %args_4_.4), custom_call_target="tpu_custom_call" | custom-call | tf_op jit(solution)/shard_map/fused/pallas_call | solution.py:432
  43.1 1.4 %spread.1 = (f32[1,1]{1,0:T(1,128)}, f32[1,1]{1,0:T(1,128)}, f32[12,320]{1,0:T(8,128)}, f32[320]{0:T(512)}) custom-call(f32[40,128]{1,0:T(8,128)} %fused.1.in_ref), custom_call_target="tpu_custom_call" | custom-call | tf_op jit(solution)/shard_map/spread/pallas_call | solution.py:479

commit v6 on v5

--- a/solution.py
+++ b/solution.py
@@ -365,8 +365,7 @@
     ) * (1.0 / NDP)
     lrow = mine[32:33, :]
     ident = me * NX + mx
-    nb[ident, 0:1] = squares
-    nb[ident, 1:2] = lrow
+    nb[ident] = jnp.where(lane < 64, squares + pltpu.roll(squares, 64, 1), lrow)
 
     def b_out(n, m):
         return pltpu.make_async_remote_copy(
@@ -396,9 +395,9 @@
     final = ((parts[0] + parts[1]) + (parts[2] + parts[3])) + (
         (parts[4] + parts[5]) + (parts[6] + parts[7])
     )
-    loss_sum = jnp.sum(jnp.where(lane == 64, final[1:2], 0.0)) * (1.0 / NDP)
+    loss_sum = jnp.sum(jnp.where(lane == 64, final, 0.0)) * (1.0 / NDP)
     count = jnp.sum(jnp.where(lane == 96, lrow, 0.0))
-    total = jnp.full((1, 128), jnp.sum(final[0:1]), F32)
+    total = jnp.full((1, 128), jnp.sum(jnp.where(lane < 64, final, 0.0)), F32)
     countv = jnp.full((1, 128), count, F32)
     norm = jnp.sqrt(total) / countv
     clip = jnp.minimum(1.0, 1.0 / (norm + 1e-06))
@@ -461,7 +460,7 @@
             vm((NCHIP, 40, 128), F32),
             vm((NCHIP, 40, 128), F32),
             vm((NCHIP, 40, 128), F32),
-            vm((NDP * NX, 2, 128), F32),
+            vm((NDP * NX, 1, 128), F32),
             dma((NG,)), dma((NG,)), dma((3,)),
             dma((NX - 1, NG)), dma((NX - 1, NG)),
             dma, dma, dma, dma, dma((NCHIP,)), dma((NCHIP,)), dma, dma, dma, dma,

time: 44.7 us -> 44.4 us (level)
  no operation moved by 1% of the time
where the time goes in v6:
time: 44.4 us; the launch traced here: 44.2 us
  Pallas kernels  43.5 us (98%)
  between operations  0.64 us (1%)
    pallas_call x1, Pallas kernels, body(): pl.pallas_call(kernel, name='fused', out_shape=jax.ShapeDtypeStruct((40,...  42.1 us
    pallas_call x1, Pallas kernels, body(): pl.pallas_call(spread, name='spread', out_shape=(jax.ShapeDtypeStruct((1,...  1.41 us

profile of v6, /device:TPU:1, one launch (start us, length us, event | category | flops | bytes accessed | tf_op | source)
XLA Modules:
  0.0 44.2 jit_solution(11167921375880875162)
XLA Ops:
  0.6 42.1 %fused.1.in_ref = f32[40,128]{1,0:T(8,128)} custom-call(bf16[64,256,384]{2,1,0:T(8,128)(2,1)} %args_0_.4, bf16[12,320]{1,0:T(8,128)(2,1)} %args_1_.4, f32[320]{0:T(512)} %args_2_.4, bf16[64,320,256]{2,1,0:T(8,128)(2,1)} %bitcast.3, s32[64,4,256]{2,1,0:T(4,128)} %args_4_.4), custom_call_target="tpu_custom_call" | custom-call | tf_op jit(solution)/shard_map/fused/pallas_call | solution.py:431
  42.8 1.4 %spread.1 = (f32[1,1]{1,0:T(1,128)}, f32[1,1]{1,0:T(1,128)}, f32[12,320]{1,0:T(8,128)}, f32[320]{0:T(512)}) custom-call(f32[40,128]{1,0:T(8,128)} %fused.1.in_ref), custom_call_target="tpu_custom_call" | custom-call | tf_op jit(solution)/shard_map/spread/pallas_call | solution.py:478

commit v7 on v6

--- a/solution.py
+++ b/solution.py
@@ -117,21 +117,6 @@
     )
     wg[core, chip] = wtmp[...].astype(BF16)
 
-    pl.semaphore_wait(barrier, (NCHIP - 1) * NC + NX)
-
-    def w_dst(n):
-        return pltpu.make_async_remote_copy(
-            src_ref=wg.at[core, chip],
-            dst_ref=wg.at[core, chip],
-            send_sem=w_send,
-            recv_sem=w_recv,
-            device_id=(n * NC + core, mx),
-            device_id_type=MESH,
-        )
-
-    for dy, dz in OFFSETS:
-        w_dst(chip_at(dy, dz)).start()
-
     b_copy.wait()
     wsq[...] = jnp.zeros_like(wsq)
     b_all = bi[...].reshape(1, FEAT)
@@ -150,6 +135,21 @@
     for piece in (*pieces, *grad):
         pltpu.matmul_pop(piece)
 
+
+    pl.semaphore_wait(barrier, (NCHIP - 1) * NC + NX)
+
+    def w_dst(n):
+        return pltpu.make_async_remote_copy(
+            src_ref=wg.at[core, chip],
+            dst_ref=wg.at[core, chip],
+            send_sem=w_send,
+            recv_sem=w_recv,
+            device_id=(n * NC + core, mx),
+            device_id_type=MESH,
+        )
+
+    for dy, dz in OFFSETS:
+        w_dst(chip_at(dy, dz)).start()
 
     lane_x = lax.broadcasted_iota(jnp.int32, (1, 1, XW - E), 2)
     ones = jnp.where(lane_x < 3, 1.0, 0.0).astype(BF16)

time: 44.4 us -> 44.3 us (level)
  no operation moved by 1% of the time
where the time goes in v7:
time: 44.3 us; the launch traced here: 44.1 us
  Pallas kernels  43.5 us (98%)
  between operations  0.64 us (1%)
    pallas_call x1, Pallas kernels, body(): pl.pallas_call(kernel, name='fused', out_shape=jax.ShapeDtypeStruct((40,...  42.1 us
    pallas_call x1, Pallas kernels, body(): pl.pallas_call(spread, name='spread', out_shape=(jax.ShapeDtypeStruct((1,...  1.41 us

profile of v7, /device:TPU:1, one launch (start us, length us, event | category | flops | bytes accessed | tf_op | source)
XLA Modules:
  0.0 44.1 jit_solution(12440439762531601775)
XLA Ops:
  0.6 42.1 %fused.1.in_ref = f32[40,128]{1,0:T(8,128)} custom-call(bf16[64,256,384]{2,1,0:T(8,128)(2,1)} %args_0_.4, bf16[12,320]{1,0:T(8,128)(2,1)} %args_1_.4, f32[320]{0:T(512)} %args_2_.4, bf16[64,320,256]{2,1,0:T(8,128)(2,1)} %bitcast.3, s32[64,4,256]{2,1,0:T(4,128)} %args_4_.4), custom_call_target="tpu_custom_call" | custom-call | tf_op jit(solution)/shard_map/fused/pallas_call | solution.py:431
  42.7 1.4 %spread.1 = (f32[1,1]{1,0:T(1,128)}, f32[1,1]{1,0:T(1,128)}, f32[12,320]{1,0:T(8,128)}, f32[320]{0:T(512)}) custom-call(f32[40,128]{1,0:T(8,128)} %fused.1.in_ref), custom_call_target="tpu_custom_call" | custom-call | tf_op jit(solution)/shard_map/spread/pallas_call | solution.py:478
